TPU v7x, 32 devices: a whole 2x2x4 slice. The times are simulated.
32 devices in a mesh: text: 4 (over y, x), graph: 8 (over z, core).
Axes of the slice: x: 2, y: 2, z: 4, core: 2. Of those that a mesh axis runs over, the one named last changes fastest.
Arguments:
- tokens: bfloat16 [16384, 768], P(('text', 'graph')), may hold values from -6 to 6
- doc_ids: int32 [128, 128], P(('text', 'graph')), may hold values from 0 to 3, never falling along the last dimension, each value on 1 to 96 neighbouring positions
- in_gain: float32 [768], replicated, may hold values from 0.25 to 1.75
- in_bias: float32 [768], replicated, may hold values from -3 to 3
- attn_qkv: bfloat16 [768, 2304], P(None, 'text'), may hold values from -0.21875 to 0.21875
- attn_out: bfloat16 [768, 768], P(None, 'text'), may hold values from -0.21875 to 0.21875
- owner_text: int32 [512, 1], P(('text', 'graph')), may hold values from 0 to 3; in each aligned block of 16 rows (0 to 15, 16 to 31, ...) at most 8 rows name the same one
- sage_one: bfloat16 [1536, 768], P('graph'), may hold values from -0.21875 to 0.21875
- sage_two: bfloat16 [1536, 768], P('graph'), may hold values from -0.21875 to 0.21875
- neighbours: int32 [1024, 15], P(('text', 'graph')), may hold values from 0 to 47
- boundary: int32 [256, 2], P(('text', 'graph')), may hold values from 0 to 31
- out_grad: bfloat16 [1024, 768], P(('text', 'graph')), may hold values from -6 to 6
Outputs:
- node_states: bfloat16 [1024, 768], P(('text', 'graph'))
- abstract_grad: bfloat16 [512, 768], P(('text', 'graph'))
Inputs may be any that keep to these rules, and one draw needn't show every extreme that they name: `doc_ids`: within each row the numbers never fall; each of the 4 numbers covers 1 to 96 positions. `owner_text`: among the 16 rows of one device no value occurs more than 8 times.
All inputs are finite; a program needn't handle non-finite values.
Results may differ from a plain program's by a relative error of at most 0.01.
Values may be sent and summed in bfloat16 or wider, within the bound.
No kernel may reach another device: no remote copies, remote signals or barrier semaphores. Data moves between devices by JAX's collectives and lax.ppermute only.
A program may use at most 64 MiB of HBM per device.

v0:
```python
import jax
import jax.numpy as jnp
from jax import lax
from jax.experimental import pallas as pl
from jax.experimental.pallas import tpu as pltpu
from jax.sharding import PartitionSpec as P

HEAD = 64
SEGS = 4
CORES = 2


epsilon = 1e-06
bf16 = jnp.bfloat16
f32 = jnp.float32


def dot(left, right, contract, batch=((), ())):
    return lax.dot_general(left, right, (contract, batch), preferred_element_type=f32)


def over_text(array, step):
    count = lax.axis_size("text")
    return lax.ppermute(array, "text", [(i, i ^ step) for i in range(count)])


def over_graph(array, step):
    count = lax.axis_size("graph")
    return lax.ppermute(array, "graph", [(i, i ^ step) for i in range(count)])


def over_pair(array, steps):
    texts, graphs = lax.axis_size("text"), lax.axis_size("graph")
    moves = []
    for t in range(texts):
        for g in range(graphs):
            moves.append((t * graphs + g, (t ^ steps[g % CORES]) * graphs + g))
    return lax.ppermute(array, ("text", "graph"), moves)


def natural(parts, own):
    stacked = jnp.stack(parts)
    return jnp.concatenate(
        [lax.dynamic_index_in_dim(stacked, own ^ j, 0, keepdims=True) for j in range(len(parts))]
    )


def fetch_text(shard, core):
    count = lax.axis_size("text")
    half = shard.shape[1] // CORES
    whole = [over_pair(shard, (k, k + 1)) for k in range(1, count - 1, 2)]
    split = lax.dynamic_slice_in_dim(shard, core * half, half, 1)
    return whole + [over_text(split, count - 1)]


def pieces_of(shard, fetched):
    return [shard] + [piece for got in fetched for piece in (got, over_graph(got, 1))]


def place_pieces(refs, whole, sem):
    text, core = lax.axis_index("text"), lax.axis_index("graph") % CORES
    rows, width = refs[0].shape
    count = whole.shape[0] // rows
    half = width // CORES
    spots = [(text, 0, width)]
    for k in range(1, count - 1, 2):
        spots += [(text ^ (k + core), 0, width), (text ^ (k + 1 - core), 0, width)]
    spots += [(text ^ (count - 1), core * half, half), (text ^ (count - 1), (1 - core) * half, half)]
    copies = []
    for i, (ref, (peer, lane, lanes)) in enumerate(zip(refs, spots)):
        at = pl.ds(pl.multiple_of(peer * rows, rows), rows)
        if lanes == width:
            target = whole.at[at, :]
        else:
            target = whole.at[at, pl.ds(pl.multiple_of(lane, half), half)]
        copies.append(pltpu.make_async_copy(ref, target, sem.at[i]))
    return copies


def assemble(pieces, text, core):
    parts = [pieces[0]]
    for got, swapped in zip(pieces[1:-2:2], pieces[2:-2:2]):
        parts.append(jnp.where(core == 0, got, swapped))
        parts.append(jnp.where(core == 0, swapped, got))
    got, swapped = pieces[-2:]
    parts.append(
        jnp.concatenate(
            [jnp.where(core == 0, got, swapped), jnp.where(core == 0, swapped, got)], axis=1
        )
    )
    return natural(parts, text).reshape(-1, parts[0].shape[1])


def gather_graph(array):
    count = lax.axis_size("graph")
    mine = jnp.stack([array] + [over_graph(array, k) for k in range(CORES, count, CORES)])
    return jnp.stack([mine, over_graph(mine, 1)], axis=1).reshape((count,) + array.shape)


def layer_norm(tokens, in_gain, in_bias):
    states = tokens.astype(f32)
    row_mean = jnp.mean(states, axis=1, keepdims=True)
    centred = states - row_mean
    variance = jnp.mean(centred * centred, axis=1, keepdims=True)
    return (centred * lax.rsqrt(variance + epsilon) * in_gain + in_bias).astype(bf16)


def attention_kernel(*refs):
    normed_ref, doc_ref, doc_column_ref = refs[:3]
    norm_out, context_out, weights, projected, raised, sem = refs[-6:]
    copies = place_pieces(refs[3:-6], weights, sem)
    for copy in copies:
        copy.start()
    width = normed_ref.shape[1]
    blocks, length = doc_ref.shape
    pair = 2 * HEAD
    lane = lax.broadcasted_iota(jnp.int32, (2 * length, pair), 1)
    row = lax.broadcasted_iota(jnp.int32, (2 * length, pair), 0)
    own_half = (lane < HEAD) == (row < length)
    scale = jnp.where(own_half, HEAD ** (-0.5), 0.0).astype(bf16)
    ones = jnp.ones((2 * SEGS, pair), bf16)
    own_head = (lax.broadcasted_iota(jnp.int32, (4 * SEGS, 2 * length), 0) < 2 * SEGS) == (
        lax.broadcasted_iota(jnp.int32, (4 * SEGS, 2 * length), 1) < length
    )
    members = []
    lengths = []
    for b in range(blocks):
        number = lax.broadcasted_iota(jnp.int32, (2 * SEGS, length), 0)
        member = jnp.where(doc_ref[b : b + 1, :] == number, 1.0, 0.0)
        count = jnp.sum(member, axis=1, keepdims=True)[:SEGS]
        members.append(jnp.concatenate([member, member]))
        lengths.append(count)
        at = slice(b * length, (b + 1) * length)
        pooled = dot(member.astype(bf16), normed_ref[at, :], ((1,), (0,)))
        norm_out[b * SEGS : (b + 1) * SEGS, :] = pooled[:SEGS] / count
    for copy in copies:
        copy.wait()
    step = 2 * pair
    for n in range(0, 3 * width, step):
        out = dot(normed_ref[...], weights[n : n + step, :], ((1,), (1,)))
        projected[:, n : n + step] = out.astype(bf16)
    for b in range(blocks):
        at = slice(b * length, (b + 1) * length)
        same = doc_column_ref[:, b : b + 1] == doc_ref[b : b + 1, :]
        same = jnp.concatenate([same, same])
        starts = range(0, width, pair)
        for i, n in enumerate(starts):
            queries = projected[at, n : n + pair]
            keys = projected[at, width + n : width + n + pair]
            scores = dot(jnp.concatenate([queries, queries]) * scale, keys, ((1,), (1,)))
            raised[i] = jnp.where(same, jnp.exp(scores), 0.0).astype(bf16)
        totals = [dot(ones, raised[i], ((1,), (1,))) for i, n in enumerate(starts)]
        shares = []
        for i, n in enumerate(starts):
            inverse = 1.0 / totals[i]
            inverse = jnp.where(own_head, jnp.concatenate([inverse, inverse]), 0.0)
            high = inverse.astype(bf16)
            low = (inverse - high.astype(f32)).astype(bf16)
            both = dot(jnp.concatenate([high, low]), raised[i], ((1,), (0,)))
            shares.append(both[: 4 * SEGS] + both[4 * SEGS :])
        for i, n in enumerate(starts):
            values = projected[at, 2 * width + n : 2 * width + n + pair]
            mixed = dot((members[b] * shares[i]).astype(bf16), values, ((1,), (0,)))
            both = jnp.where(lane[: 2 * SEGS] < HEAD, mixed[: 2 * SEGS], mixed[2 * SEGS :])
            context_out[b * SEGS : (b + 1) * SEGS, n : n + pair] = both[:SEGS] / lengths[b]


def attention(normed, doc_ids, pieces):
    tokens, width = normed.shape
    blocks, length = doc_ids.shape
    vmem, anywhere = pl.BlockSpec(memory_space=pltpu.VMEM), pl.BlockSpec(memory_space=pl.ANY)
    pooled = jax.ShapeDtypeStruct((blocks * SEGS, width), f32)
    flops = 2 * tokens * width * 3 * width + 6 * tokens * length * width
    return pl.pallas_call(
        attention_kernel,
        out_shape=(pooled, pooled),
        in_specs=[vmem] * 3 + [anywhere] * len(pieces),
        out_specs=(vmem, vmem),
        scratch_shapes=[
            pltpu.VMEM((3 * width, width), bf16),
            pltpu.VMEM((tokens, 3 * width), bf16),
            pltpu.VMEM((width // (2 * HEAD), 2 * length, length), bf16),
            pltpu.SemaphoreType.DMA((len(pieces),)),
        ],
        cost_estimate=pl.CostEstimate(
            flops=flops, bytes_accessed=8 * width * width, transcendentals=tokens * length * width // HEAD
        ),
        name="attention",
    )(normed, doc_ids, doc_ids.T, *pieces)


def local(
    tokens,
    doc_ids,
    in_gain,
    in_bias,
    attn_qkv,
    attn_out,
    owner_text,
    sage_one,
    sage_two,
    neighbours,
    boundary,
    out_grad,
):
    width = tokens.shape[1]
    texts, graphs = lax.axis_size("text"), lax.axis_size("graph")
    text, graph = lax.axis_index("text"), lax.axis_index("graph")
    core, z = graph % CORES, graph // CORES
    rows = out_grad.shape[0]
    made = owner_text.shape[0]
    capacity = rows // texts
    fan = neighbours.shape[1]
    slot_count = boundary.shape[1]
    i32 = jnp.int32

    qkv_shard, out_shard = attn_qkv.T, attn_out.T
    qkv_fetched = fetch_text(qkv_shard, core)
    out_fetched = fetch_text(out_shard, core)
    qkv_pieces = pieces_of(qkv_shard, qkv_fetched)
    out_pieces = pieces_of(out_shard, out_fetched)

    depth = sage_one.shape[0]
    share = depth // texts
    hidden = (graphs // 2) * share
    lanes = next(n for n in range(128, width + 1, 128) if n >= hidden and width % n == 0)
    column = jnp.arange(lanes, dtype=i32)
    wanted = (column // share) * depth + text * share + column % share
    wanted = jnp.where(column < hidden, wanted, -1)
    chosen = (jnp.arange(width, dtype=i32)[:, None] == wanted[None, :]).astype(bf16)
    one_share = dot(sage_one, chosen, ((1,), (0,))).astype(bf16)
    two_share = lax.dynamic_slice_in_dim(sage_two, text * share, share, 0)
    packed = jnp.concatenate(
        [one_share] + [two_share[:, i : i + lanes] for i in range(0, width, lanes)], axis=0
    )
    got = gather_graph(packed)
    got = natural(
        [got[CORES * k : CORES * (k + 1)] for k in range(graphs // CORES)], z
    )
    got = jnp.where(core == 0, got, got[:, ::-1]).reshape(graphs, -1, lanes)
    one = got[:, :depth].reshape(2, width, lanes)
    two = got[:, depth:].reshape(2, hidden // share, width // lanes, share, lanes)
    two = two.transpose(0, 1, 3, 2, 4).reshape(2, hidden, width)
    one = one[:, :, :hidden]

    facts = jnp.concatenate(
        [neighbours.reshape(-1), boundary.reshape(-1), owner_text.reshape(-1)]
    ).astype(bf16)
    fact_count = facts.shape[0]
    fact_rows = -(-fact_count // width)
    facts = jnp.pad(facts, (0, fact_rows * width - fact_count)).reshape(fact_rows, width)
    outset = jnp.concatenate([out_grad, facts], axis=0)
    outset = jnp.stack([outset] + [over_text(outset, k) for k in range(1, texts)])
    grads = outset[:, :rows]
    facts = outset[:, rows:].reshape(texts, -1)[:, :fact_count]

    def slot_places(owners):
        same = owners[..., :, None] == owners[..., None, :]
        order = jnp.arange(made, dtype=i32)
        earlier = jnp.sum((same & (order[None, :] < order[:, None])).astype(i32), axis=-1)
        source = text ^ jnp.arange(texts, dtype=i32)
        place = (owners ^ text) * rows + source[:, None] * capacity + earlier
        return place.reshape(owners.shape[:-2] + (1, texts * made))

    own_places = slot_places(facts[:, fact_count - made :].astype(i32))
    own_table = (own_places == jnp.arange(texts * rows, dtype=i32)[:, None]).astype(bf16)
    wide = 2 * hidden
    all_count = texts * fact_count
    all_rows = -(-all_count // width)
    flat = jnp.pad(facts.reshape(-1), (0, all_rows * width - all_count)).reshape(all_rows, width)
    facts = gather_graph(flat).reshape(graphs, -1)[:, :all_count]
    facts = facts.reshape(graphs, texts, fact_count).astype(i32)

    listed = facts[..., : rows * fan].reshape(graphs, texts, rows, fan)
    bounds = facts[..., rows * fan : fact_count - made].reshape(graphs, texts, graphs, slot_count)
    owners = facts[..., fact_count - made :]
    places = slot_places(owners)
    peer = graph ^ jnp.arange(graphs, dtype=i32)
    halo_name = (rows + peer[:, None] * slot_count + jnp.arange(slot_count, dtype=i32)).reshape(-1)
    extended_name = jnp.concatenate([jnp.arange(rows, dtype=i32), halo_name])
    turned = (jnp.arange(graphs, dtype=i32)[:, None] == peer[None, :]).astype(f32)
    halo_row = jnp.einsum("ptgk,gd->tdpk", bounds.astype(f32), turned).astype(i32)
    halo_row = halo_row.reshape(texts, graphs, graphs * slot_count)
    halo_at = jnp.repeat(jnp.arange(graphs, dtype=i32), slot_count) * rows + halo_row
    nodes = graphs * rows

    def node_stage(one_text):
        distance, listed, halo_at = one_text
        counts = jnp.sum((listed[..., None] == extended_name).astype(f32), axis=2).astype(bf16)
        table = (places == distance * rows + jnp.arange(rows, dtype=i32)[:, None]).astype(bf16)
        live = jnp.sum(table.astype(f32), axis=2).reshape(nodes, 1)

        def to_rows(by_abstract):
            return dot(table, by_abstract, ((2,), (1,)), ((0,), (0,))).reshape(nodes, -1)

        if dense:
            self_at = jnp.arange(nodes, dtype=i32).reshape(graphs, rows)
            at = jnp.concatenate([self_at, halo_at], axis=1)
            place = (at[..., None] == jnp.arange(nodes, dtype=i32)).astype(bf16)
            links = dot(counts, place, ((2,), (1,)), ((0,), (0,)))
            links = links.astype(bf16).reshape(nodes, nodes)

            def pull(values, count):
                return dot(links[:count], values, ((1,), (0,)))

            def push(values, count):
                return dot(links[:, :count], values, ((0,), (0,)))

        else:
            halo = halo_at.reshape(-1)

            def pull(values, count):
                outer = values[halo].reshape(graphs, -1, values.shape[1])
                inner = values.reshape(graphs, rows, -1)
                extended = jnp.concatenate([inner, outer], axis=1)
                out = dot(counts, extended, ((2,), (1,)), ((0,), (0,)))
                return out.reshape(nodes, -1)[:count]

            def push(values, count):
                out = dot(counts, values.reshape(graphs, rows, -1), ((1,), (1,)), ((0,), (0,)))
                inner = out[:, :rows].reshape(nodes, -1)
                return inner.at[halo].add(out[:, rows:].reshape(halo.shape[0], -1))[:count]

        up_rows = to_rows(ups)
        into_one = up_rows[:, :hidden] + push(up_rows[:, hidden:].astype(bf16), nodes) / fan
        first_rows = to_rows(firsts)
        preact_one = first_rows[:, :hidden] + pull(first_rows[:, hidden:].astype(bf16), nodes) / fan
        gelu_value, pull_back = jax.vjp(jax.nn.gelu, preact_one)
        hidden_one = (live * gelu_value).astype(bf16)
        grad_one = (live * pull_back(into_one)[0]).astype(bf16)
        aggregated = (pull(hidden_one, rows) / fan).astype(bf16)
        returned = (push(grad_one, rows) / fan).astype(bf16)
        return (
            jnp.concatenate([hidden_one[:rows], aggregated], axis=1),
            jnp.concatenate([grad_one[:rows], returned], axis=1),
            live[:rows],
        )

    normed = layer_norm(tokens, in_gain, in_bias)
    pooled_norm, pooled_context = attention(normed, doc_ids, qkv_pieces)
    out_proj = assemble(out_pieces, text, core)
    embedded = dot(pooled_context.astype(bf16), out_proj, ((1,), (1,)))
    embedded = (pooled_norm + embedded).astype(bf16)
    grads, embedded = lax.optimization_barrier((grads, embedded))
    live_grad = dot(own_table, grads.reshape(texts * rows, width), ((0,), (0,))).astype(bf16)
    up = jnp.concatenate(
        [dot(live_grad, two[0], ((1,), (1,))), dot(live_grad, two[1], ((1,), (1,)))], axis=1
    ).astype(bf16)
    ups = gather_graph(up)
    gathered = jnp.concatenate(
        [embedded] + [over_text(embedded, k) for k in range(1, texts)], axis=0
    )
    first = jnp.concatenate(
        [dot(gathered, one[0], ((1,), (0,))), dot(gathered, one[1], ((1,), (0,)))], axis=1
    ).astype(bf16)
    firsts = gather_graph(first)

    dense = texts * graphs <= 64
    per_text = (jnp.arange(texts, dtype=i32), listed.transpose(1, 0, 2, 3), halo_at)
    if dense:
        forth, back, live = jax.vmap(node_stage)(per_text)
    else:
        forth, back, live = lax.map(node_stage, per_text)
    forth = forth.reshape(texts * rows, wide)
    state_part = dot(forth[:, :hidden], two[0], ((1,), (0,))) + dot(
        forth[:, hidden:], two[1], ((1,), (0,))
    )
    back = dot(own_table, back.reshape(texts * rows, wide), ((0,), (0,))).astype(bf16)
    grad_part = dot(back[:, :hidden], one[0], ((1,), (1,))) + dot(
        back[:, hidden:], one[1], ((1,), (1,))
    )

    final = jnp.concatenate(
        [state_part.reshape(texts, rows, width), grad_part.reshape(texts, made, width)], axis=1
    )
    total = final[0]
    outgoing = final.astype(bf16)
    for k in range(1, texts):
        total = total + over_text(outgoing[k], k).astype(f32)
    node_states = (live[0] * total[:rows]).astype(bf16)
    return (node_states, total[rows:].astype(bf16))


def solution(mesh):
    rowwise = P(("text", "graph"), None)
    placed = (
        rowwise,
        rowwise,
        P(),
        P(),
        P(None, "text"),
        P(None, "text"),
        rowwise,
        P("graph", None),
        P("graph", None),
        rowwise,
        rowwise,
        rowwise,
    )

    return jax.shard_map(
        local, mesh=mesh, in_specs=placed, out_specs=(rowwise, rowwise), check_vma=False
    )
```

profile of v0, /device:TPU:0, one launch (start us, length us, event | category | flops | bytes accessed | tf_op | source)
XLA Modules:
  0.0 111.0 jit_solution(3629965823151050432)
XLA Ops:
  2.8 5.1 %collective-permute-start.20 = (bf16[336,256]{1,0:T(8,128)(2,1)S(1)}, bf16[336,256]{1,0:T(8,128)(2,1)S(1)}, u32[]{:S(2)}, u32[]{:S(2)}) collective-permute-start(bf16[336,256]{1,0:T(8,128)(2,1)S(1)} %get-tuple-element.33), channel_id=1, source_target_pairs={{0,6},{1,7},{2,4},{3,5},{4,2},{5,3},{6,0},{7,1},{8,14},{9,15},{10,... | collective-permute-start | bytes 516104 | tf_op jit(solution)/shard_map/ppermute | solution.py:29
  9.3 2.5 %collective-permute-start.2 = (bf16[33,768]{1,0:T(8,128)(2,1)S(1)}, bf16[33,768]{1,0:T(8,128)(2,1)S(1)}, u32[]{:S(2)}, u32[]{:S(2)}) collective-permute-start(bf16[33,768]{1,0:T(8,128)(2,1)S(1)} %constant_dynamic-update-slice_fusion), channel_id=1, source_target_pairs={{0,24},{8,16},{16,8},{24,0},{1,25},{9,17},{17,9},{25,1},{2,26},{10... | collective-permute-start | bytes 152072 | tf_op jit(solution)/shard_map/ppermute | solution.py:24
  14.5 1.2 %fusion.5.refs_0_ = bf16[512,768]{1,0:T(8,128)(2,1)} fusion(bf16[512,768]{1,0:T(8,128)(2,1)S(1)} %copy-done.1, f32[768]{0:T(1024)S(1)} %copy-done.8, f32[768]{0:T(1024)S(1)} %copy-done.9, f32[512]{0:T(512)S(1)} %add_rsqrt_fusion, f32[512]{0:T(512)S(1)} %broadcast_multiply_fusion), kind=kLoop, calls=%fused_computation.17 | loop fusion | flops 2359296 | bytes 1583104 | tf_op jit(solution)/shard_map/convert_element_type | solution.py:105
  16.7 2.0 %collective-permute-start.5 = (bf16[3,768]{1,0:T(4,128)(2,1)S(1)}, bf16[3,768]{1,0:T(4,128)(2,1)S(1)}, u32[]{:S(2)}, u32[]{:S(2)}) collective-permute-start(bf16[3,768]{1,0:T(4,128)(2,1)S(1)} %reshape.312), channel_id=1, source_target_pairs={{0,6},{1,7},{2,4},{3,5},{4,2},{5,3},{6,0},{7,1},{8,14},{9,15},{10,... | collective-permute-start | bytes 13832 | tf_op jit(solution)/shard_map/ppermute | solution.py:29
  19.8 1.4 %collective-permute-start.3 = (bf16[3,768]{1,0:T(4,128)(2,1)S(1)}, bf16[3,768]{1,0:T(4,128)(2,1)S(1)}, u32[]{:S(2)}, u32[]{:S(2)}) collective-permute-start(bf16[3,768]{1,0:T(4,128)(2,1)S(1)} %reshape.312), channel_id=1, source_target_pairs={{0,2},{1,3},{2,0},{3,1},{4,6},{5,7},{6,4},{7,5},{8,10},{9,11},{10,... | collective-permute-start | bytes 13832 | tf_op jit(solution)/shard_map/ppermute | solution.py:29
  23.5 2.4 %collective-permute-start.13 = (bf16[192,384]{1,0:T(8,128)(2,1)}, bf16[192,384]{1,0:T(8,128)(2,1)}, u32[]{:S(2)}, u32[]{:S(2)}) collective-permute-start(bf16[192,384]{1,0:T(8,128)(2,1)} %dynamic-slice_bitcast_fusion.1), channel_id=1, source_target_pairs={{0,24},{8,16},{16,8},{24,0},{1,25},{9,17},{17,9},{25,1},{2,26},{10... | collective-permute-start | bytes 442376 | tf_op jit(solution)/shard_map/ppermute | solution.py:24
  30.2 3.2 %convert_reduce_fusion = bf16[4,8,32,48]{3,2,1,0:T(8,128)(2,1)S(1)} fusion(s32[48]{0:T(128)S(1)} %pad_add_fusion.1, s32[4,8,32,15]{2,3,1,0:T(8,128)S(1)} %copy.162), kind=kLoop, calls=%fused_computation | loop fusion | flops 2162688 | bytes 159936 | tf_op jit(solution)/shard_map/vmap()/reduce_sum | solution.py:289
  33.5 1.2 %fusion.9 = bf16[4,8,32,256]{3,2,1,0:T(8,128)(2,1)} fusion(s32[4,8,48]{2,1,0:T(8,128)S(1)} %pad_add_fusion, bf16[4,8,32,48]{3,2,1,0:T(8,128)(2,1)S(1)} %convert_reduce_fusion), kind=kOutput, calls=%fused_computation.27 | convolution fusion | flops 25821184 | bytes 628736 | tf_op jit(solution)/shard_map/vmap()/dot_general | solution.py:19
  35.3 1.5 %collective-permute-start.7 = (bf16[576,768]{1,0:T(8,128)(2,1)}, bf16[576,768]{1,0:T(8,128)(2,1)S(1)}, u32[]{:S(2)}, u32[]{:S(2)}) collective-permute-start(bf16[576,768]{1,0:T(8,128)(2,1)} %bitcast.209), channel_id=1, source_target_pairs={{0,8},{1,17},{2,10},{3,19},{4,12},{5,21},{6,14},{7,23},{8,0},{9,25... | collective-permute-start | bytes 2654216 | tf_op jit(solution)/shard_map/ppermute | solution.py:38
  36.8 1.3 %collective-permute-start.9 = (bf16[576,384]{1,0:T(8,128)(2,1)S(1)}, bf16[576,384]{1,0:T(8,128)(2,1)S(1)}, u32[]{:S(2)}, u32[]{:S(2)}) collective-permute-start(bf16[576,384]{1,0:T(8,128)(2,1)S(1)} %dynamic-slice_bitcast_fusion), channel_id=1, source_target_pairs={{0,24},{8,16},{16,8},{24,0},{1,25},{9,17},{17,9},{25,1},{2,26},{10... | collective-permute-start | bytes 1327112 | tf_op jit(solution)/shard_map/ppermute | solution.py:24
  40.8 18.1 %collective-permute-done.9.refs_6_ = bf16[576,384]{1,0:T(8,128)(2,1)S(1)} collective-permute-done((bf16[576,384]{1,0:T(8,128)(2,1)S(1)}, bf16[576,384]{1,0:T(8,128)(2,1)S(1)}, u32[]{:S(2)}, u32[]{:S(2)}) %collective-permute-start.9) | collective-permute-done | bytes 442400 | tf_op jit(solution)/shard_map/ppermute | solution.py:24
  63.2 7.9 %attention.1 = (f32[16,768]{1,0:T(8,128)}, f32[16,768]{1,0:T(8,128)}) custom-call(bf16[512,768]{1,0:T(8,128)(2,1)} %fusion.5.refs_0_, s32[4,128]{1,0:T(4,128)} %refs_1_.1, s32[128,4]{1,0:T(8,128)} %bitcast.234, bf16[576,768]{1,0:T(8,128)(2,1)} %bitcast.210, bf16[576,768]{1,0:T(8,128)(2,1)} %copy-done.11, bf16[576,768]{1,0:T(8,128)(2,1)} %copy-done.12, ...), custom_call_target="tpu_custom_call" | custom-call | flops 2113929216 | bytes 4718592 | tf_op jit(solution)/shard_map/attention/pallas_call | solution.py:174
  73.9 1.5 %collective-permute-start.16 = (bf16[16,768]{1,0:T(8,128)(2,1)S(1)}, bf16[16,768]{1,0:T(8,128)(2,1)S(1)}, u32[]{:S(2)}, u32[]{:S(2)}) collective-permute-start(bf16[16,768]{1,0:T(8,128)(2,1)S(1)} %add_convert_fusion), channel_id=1, source_target_pairs={{0,16},{8,24},{16,0},{24,8},{1,17},{9,25},{17,1},{25,9},{2,18},{10... | collective-permute-start | bytes 73736 | tf_op jit(solution)/shard_map/ppermute | solution.py:24
  75.4 1.3 %collective-permute-start.17 = (bf16[16,768]{1,0:T(8,128)(2,1)S(1)}, bf16[16,768]{1,0:T(8,128)(2,1)S(1)}, u32[]{:S(2)}, u32[]{:S(2)}) collective-permute-start(bf16[16,768]{1,0:T(8,128)(2,1)S(1)} %add_convert_fusion), channel_id=1, source_target_pairs={{0,24},{8,16},{16,8},{24,0},{1,25},{9,17},{17,9},{25,1},{2,26},{10... | collective-permute-start | bytes 73736 | tf_op jit(solution)/shard_map/ppermute | solution.py:24
  77.5 2.6 %collective-permute-start.28 = (bf16[64,384]{1,0:T(8,128)(2,1)S(1)}, bf16[64,384]{1,0:T(8,128)(2,1)S(1)}, u32[]{:S(2)}, u32[]{:S(2)}) collective-permute-start(bf16[64,384]{1,0:T(8,128)(2,1)S(1)} %pad_maximum_fusion.17), channel_id=1, source_target_pairs={{0,6},{1,7},{2,4},{3,5},{4,2},{5,3},{6,0},{7,1},{8,14},{9,15},{10,... | collective-permute-start | bytes 147464 | tf_op jit(solution)/shard_map/ppermute | solution.py:29
  80.3 1.6 %collective-permute-start.26 = (bf16[64,384]{1,0:T(8,128)(2,1)S(1)}, bf16[64,384]{1,0:T(8,128)(2,1)S(1)}, u32[]{:S(2)}, u32[]{:S(2)}) collective-permute-start(bf16[64,384]{1,0:T(8,128)(2,1)S(1)} %pad_maximum_fusion.17), channel_id=1, source_target_pairs={{0,2},{1,3},{2,0},{3,1},{4,6},{5,7},{6,4},{7,5},{8,10},{9,11},{10,... | collective-permute-start | bytes 147464 | tf_op jit(solution)/shard_map/ppermute | solution.py:29
  82.5 2.6 %collective-permute-start.24 = (bf16[64,384]{1,0:T(8,128)(2,1)S(1)}, bf16[64,384]{1,0:T(8,128)(2,1)S(1)}, u32[]{:S(2)}, u32[]{:S(2)}) collective-permute-start(bf16[64,384]{1,0:T(8,128)(2,1)S(1)} %pad_maximum_fusion.16), channel_id=1, source_target_pairs={{0,6},{1,7},{2,4},{3,5},{4,2},{5,3},{6,0},{7,1},{8,14},{9,15},{10,... | collective-permute-start | bytes 147464 | tf_op jit(solution)/shard_map/ppermute | solution.py:29
  85.1 1.8 %collective-permute-start.22 = (bf16[64,384]{1,0:T(8,128)(2,1)S(1)}, bf16[64,384]{1,0:T(8,128)(2,1)S(1)}, u32[]{:S(2)}, u32[]{:S(2)}) collective-permute-start(bf16[64,384]{1,0:T(8,128)(2,1)S(1)} %pad_maximum_fusion.16), channel_id=1, source_target_pairs={{0,2},{1,3},{2,0},{3,1},{4,6},{5,7},{6,4},{7,5},{8,10},{9,11},{10,... | collective-permute-start | bytes 147464 | tf_op jit(solution)/shard_map/ppermute | solution.py:29
  87.2 1.9 %collective-permute-done.24 = bf16[64,384]{1,0:T(8,128)(2,1)S(1)} collective-permute-done((bf16[64,384]{1,0:T(8,128)(2,1)S(1)}, bf16[64,384]{1,0:T(8,128)(2,1)S(1)}, u32[]{:S(2)}, u32[]{:S(2)}) %collective-permute-start.24) | collective-permute-done | bytes 49184 | tf_op jit(solution)/shard_map/ppermute | solution.py:29
  97.4 2.0 %multiply_convert_fusion = (bf16[4,256,192]{1,2,0:T(8,128)(2,1)S(1)}, f32[4,256,192]{1,2,0:T(8,128)S(1)}) fusion(f32[4,256]{1,0:T(4,128)S(1)} %mul.160, f32[4,256,192]{1,2,0:T(8,128)} %copy.181, bf16[4,256,256]{2,1,0:T(8,128)(2,1)} %bitcast.211, bf16[4,256,192]{1,2,0:T(8,128)(2,1)S(1)} %copy.182), kind=kOutput, calls=%fused_computation.60 | convolution fusion | flops 103022592 | bytes 2887680 | tf_op jit(solution)/shard_map/vmap()/dot_general | solution.py:19
  102.4 1.6 %collective-permute-start.32 = (bf16[48,768]{1,0:T(8,128)(2,1)S(1)}, bf16[48,768]{1,0:T(8,128)(2,1)S(1)}, u32[]{:S(2)}, u32[]{:S(2)}) collective-permute-start(bf16[48,768]{1,0:T(8,128)(2,1)S(1)} %get-tuple-element.25), channel_id=1, source_target_pairs={{0,24},{8,16},{16,8},{24,0},{1,25},{9,17},{17,9},{25,1},{2,26},{10... | collective-permute-start | bytes 221192 | tf_op jit(solution)/shard_map/ppermute | solution.py:24
  104.6 1.4 %collective-permute-start.30 = (bf16[48,768]{1,0:T(8,128)(2,1)S(1)}, bf16[48,768]{1,0:T(8,128)(2,1)S(1)}, u32[]{:S(2)}, u32[]{:S(2)}) collective-permute-start(bf16[48,768]{1,0:T(8,128)(2,1)S(1)} %get-tuple-element.24), channel_id=1, source_target_pairs={{0,8},{8,0},{16,24},{24,16},{1,9},{9,1},{17,25},{25,17},{2,10},{10... | collective-permute-start | bytes 221192 | tf_op jit(solution)/shard_map/ppermute | solution.py:24
  106.0 2.2 %collective-permute-done.32 = bf16[48,768]{1,0:T(8,128)(2,1)S(1)} collective-permute-done((bf16[48,768]{1,0:T(8,128)(2,1)S(1)}, bf16[48,768]{1,0:T(8,128)(2,1)S(1)}, u32[]{:S(2)}, u32[]{:S(2)}) %collective-permute-start.32) | collective-permute-done | bytes 73760 | tf_op jit(solution)/shard_map/ppermute | solution.py:24
  108.2 1.5 %collective-permute-done.31 = bf16[48,768]{1,0:T(8,128)(2,1)S(1)} collective-permute-done((bf16[48,768]{1,0:T(8,128)(2,1)S(1)}, bf16[48,768]{1,0:T(8,128)(2,1)S(1)}, u32[]{:S(2)}, u32[]{:S(2)}) %collective-permute-start.31) | collective-permute-done | bytes 73760 | tf_op jit(solution)/shard_map/ppermute | solution.py:24
  (221 shorter events, 39.4 us)
Async XLA Ops:
  2.8 32.5 %collective-permute-start.20 = (bf16[336,256]{1,0:T(8,128)(2,1)S(1)}, bf16[336,256]{1,0:T(8,128)(2,1)S(1)}, u32[]{:S(2)}, u32[]{:S(2)}) collective-permute-start(bf16[336,256]{1,0:T(8,128)(2,1)S(1)} %get-tuple-element.33), channel_id=1, source_target_pairs={{0,6},{1,7},{2,4},{3,5},{4,2},{5,3},{6,0},{7,1},{8,14},{9,15},{10,... | collective-permute-start | bytes 516104 | tf_op jit(solution)/shard_map/ppermute | solution.py:29
  8.0 28.9 %collective-permute-start.19 = (bf16[336,256]{1,0:T(8,128)(2,1)S(1)}, bf16[336,256]{1,0:T(8,128)(2,1)}, u32[]{:S(2)}, u32[]{:S(2)}) collective-permute-start(bf16[336,256]{1,0:T(8,128)(2,1)S(1)} %get-tuple-element.33), channel_id=1, source_target_pairs={{0,4},{1,5},{2,6},{3,7},{4,0},{5,1},{6,2},{7,3},{8,12},{9,13},{10,... | collective-permute-start | bytes 516104 | tf_op jit(solution)/shard_map/ppermute | solution.py:29
  9.3 7.3 %collective-permute-start.2 = (bf16[33,768]{1,0:T(8,128)(2,1)S(1)}, bf16[33,768]{1,0:T(8,128)(2,1)S(1)}, u32[]{:S(2)}, u32[]{:S(2)}) collective-permute-start(bf16[33,768]{1,0:T(8,128)(2,1)S(1)} %constant_dynamic-update-slice_fusion), channel_id=1, source_target_pairs={{0,24},{8,16},{16,8},{24,0},{1,25},{9,17},{17,9},{25,1},{2,26},{10... | collective-permute-start | bytes 152072 | tf_op jit(solution)/shard_map/ppermute | solution.py:24
  16.7 5.6 %collective-permute-start.5 = (bf16[3,768]{1,0:T(4,128)(2,1)S(1)}, bf16[3,768]{1,0:T(4,128)(2,1)S(1)}, u32[]{:S(2)}, u32[]{:S(2)}) collective-permute-start(bf16[3,768]{1,0:T(4,128)(2,1)S(1)} %reshape.312), channel_id=1, source_target_pairs={{0,6},{1,7},{2,4},{3,5},{4,2},{5,3},{6,0},{7,1},{8,14},{9,15},{10,... | collective-permute-start | bytes 13832 | tf_op jit(solution)/shard_map/ppermute | solution.py:29
  19.8 6.2 %collective-permute-start.3 = (bf16[3,768]{1,0:T(4,128)(2,1)S(1)}, bf16[3,768]{1,0:T(4,128)(2,1)S(1)}, u32[]{:S(2)}, u32[]{:S(2)}) collective-permute-start(bf16[3,768]{1,0:T(4,128)(2,1)S(1)} %reshape.312), channel_id=1, source_target_pairs={{0,2},{1,3},{2,0},{3,1},{4,6},{5,7},{6,4},{7,5},{8,10},{9,11},{10,... | collective-permute-start | bytes 13832 | tf_op jit(solution)/shard_map/ppermute | solution.py:29
  22.3 15.8 %collective-permute-start.18 = (bf16[336,256]{1,0:T(8,128)(2,1)S(1)}, bf16[336,256]{1,0:T(8,128)(2,1)S(1)}, u32[]{:S(2)}, u32[]{:S(2)}) collective-permute-start(bf16[336,256]{1,0:T(8,128)(2,1)S(1)} %get-tuple-element.33), channel_id=1, source_target_pairs={{0,2},{1,3},{2,0},{3,1},{4,6},{5,7},{6,4},{7,5},{8,10},{9,11},{10,... | collective-permute-start | bytes 516104 | tf_op jit(solution)/shard_map/ppermute | solution.py:29
  23.5 11.3 %collective-permute-start.13 = (bf16[192,384]{1,0:T(8,128)(2,1)}, bf16[192,384]{1,0:T(8,128)(2,1)}, u32[]{:S(2)}, u32[]{:S(2)}) collective-permute-start(bf16[192,384]{1,0:T(8,128)(2,1)} %dynamic-slice_bitcast_fusion.1), channel_id=1, source_target_pairs={{0,24},{8,16},{16,8},{24,0},{1,25},{9,17},{17,9},{25,1},{2,26},{10... | collective-permute-start | bytes 442376 | tf_op jit(solution)/shard_map/ppermute | solution.py:24
  27.2 12.1 %collective-permute-start.11 = (bf16[192,768]{1,0:T(8,128)(2,1)S(1)}, bf16[192,768]{1,0:T(8,128)(2,1)S(1)}, u32[]{:S(2)}, u32[]{:S(2)}) collective-permute-start(bf16[192,768]{1,0:T(8,128)(2,1)S(1)} %bitcast.187), channel_id=1, source_target_pairs={{0,8},{1,17},{2,10},{3,19},{4,12},{5,21},{6,14},{7,23},{8,0},{9,25... | collective-permute-start | bytes 884744 | tf_op jit(solution)/shard_map/ppermute | solution.py:38
  35.3 24.4 %collective-permute-start.7 = (bf16[576,768]{1,0:T(8,128)(2,1)}, bf16[576,768]{1,0:T(8,128)(2,1)S(1)}, u32[]{:S(2)}, u32[]{:S(2)}) collective-permute-start(bf16[576,768]{1,0:T(8,128)(2,1)} %bitcast.209), channel_id=1, source_target_pairs={{0,8},{1,17},{2,10},{3,19},{4,12},{5,21},{6,14},{7,23},{8,0},{9,25... | collective-permute-start | bytes 2654216 | tf_op jit(solution)/shard_map/ppermute | solution.py:38
  36.8 22.0 %collective-permute-start.9 = (bf16[576,384]{1,0:T(8,128)(2,1)S(1)}, bf16[576,384]{1,0:T(8,128)(2,1)S(1)}, u32[]{:S(2)}, u32[]{:S(2)}) collective-permute-start(bf16[576,384]{1,0:T(8,128)(2,1)S(1)} %dynamic-slice_bitcast_fusion), channel_id=1, source_target_pairs={{0,24},{8,16},{16,8},{24,0},{1,25},{9,17},{17,9},{25,1},{2,26},{10... | collective-permute-start | bytes 1327112 | tf_op jit(solution)/shard_map/ppermute | solution.py:24
  39.2 20.8 %collective-permute-start.21 = (bf16[4,336,256]{2,1,0:T(8,128)(2,1)S(1)}, bf16[4,336,256]{2,1,0:T(8,128)(2,1)S(1)}, u32[]{:S(2)}, u32[]{:S(2)}) collective-permute-start(bf16[4,336,256]{2,1,0:T(8,128)(2,1)S(1)} %get-tuple-element.20), channel_id=1, source_target_pairs={{0,1},{1,0},{2,3},{3,2},{4,5},{5,4},{6,7},{7,6},{8,9},{9,8},{10,11... | collective-permute-start | bytes 2064392 | tf_op jit(solution)/shard_map/ppermute | solution.py:29
  39.3 19.5 %collective-permute-start.12 = (bf16[192,768]{1,0:T(8,128)(2,1)S(1)}, bf16[192,768]{1,0:T(8,128)(2,1)S(1)}, u32[]{:S(2)}, u32[]{:S(2)}) collective-permute-start(bf16[192,768]{1,0:T(8,128)(2,1)S(1)} %collective-permute-done.11), channel_id=1, source_target_pairs={{0,1},{1,0},{2,3},{3,2},{4,5},{5,4},{6,7},{7,6},{8,9},{9,8},{10,11... | collective-permute-start | bytes 884744 | tf_op jit(solution)/shard_map/ppermute | solution.py:29
  73.2 7.2 %collective-permute-start.15 = (bf16[16,768]{1,0:T(8,128)(2,1)S(1)}, bf16[16,768]{1,0:T(8,128)(2,1)S(1)}, u32[]{:S(2)}, u32[]{:S(2)}) collective-permute-start(bf16[16,768]{1,0:T(8,128)(2,1)S(1)} %add_convert_fusion), channel_id=1, source_target_pairs={{0,8},{8,0},{16,24},{24,16},{1,9},{9,1},{17,25},{25,17},{2,10},{10... | collective-permute-start | bytes 73736 | tf_op jit(solution)/shard_map/ppermute | solution.py:24
  73.9 8.1 %collective-permute-start.16 = (bf16[16,768]{1,0:T(8,128)(2,1)S(1)}, bf16[16,768]{1,0:T(8,128)(2,1)S(1)}, u32[]{:S(2)}, u32[]{:S(2)}) collective-permute-start(bf16[16,768]{1,0:T(8,128)(2,1)S(1)} %add_convert_fusion), channel_id=1, source_target_pairs={{0,16},{8,24},{16,0},{24,8},{1,17},{9,25},{17,1},{25,9},{2,18},{10... | collective-permute-start | bytes 73736 | tf_op jit(solution)/shard_map/ppermute | solution.py:24
  75.4 6.6 %collective-permute-start.17 = (bf16[16,768]{1,0:T(8,128)(2,1)S(1)}, bf16[16,768]{1,0:T(8,128)(2,1)S(1)}, u32[]{:S(2)}, u32[]{:S(2)}) collective-permute-start(bf16[16,768]{1,0:T(8,128)(2,1)S(1)} %add_convert_fusion), channel_id=1, source_target_pairs={{0,24},{8,16},{16,8},{24,0},{1,25},{9,17},{17,9},{25,1},{2,26},{10... | collective-permute-start | bytes 73736 | tf_op jit(solution)/shard_map/ppermute | solution.py:24
  77.5 7.6 %collective-permute-start.28 = (bf16[64,384]{1,0:T(8,128)(2,1)S(1)}, bf16[64,384]{1,0:T(8,128)(2,1)S(1)}, u32[]{:S(2)}, u32[]{:S(2)}) collective-permute-start(bf16[64,384]{1,0:T(8,128)(2,1)S(1)} %pad_maximum_fusion.17), channel_id=1, source_target_pairs={{0,6},{1,7},{2,4},{3,5},{4,2},{5,3},{6,0},{7,1},{8,14},{9,15},{10,... | collective-permute-start | bytes 147464 | tf_op jit(solution)/shard_map/ppermute | solution.py:29
  80.1 6.8 %collective-permute-start.27 = (bf16[64,384]{1,0:T(8,128)(2,1)S(1)}, bf16[64,384]{1,0:T(8,128)(2,1)S(1)}, u32[]{:S(2)}, u32[]{:S(2)}) collective-permute-start(bf16[64,384]{1,0:T(8,128)(2,1)S(1)} %pad_maximum_fusion.17), channel_id=1, source_target_pairs={{0,4},{1,5},{2,6},{3,7},{4,0},{5,1},{6,2},{7,3},{8,12},{9,13},{10,... | collective-permute-start | bytes 147464 | tf_op jit(solution)/shard_map/ppermute | solution.py:29
  80.3 6.6 %collective-permute-start.26 = (bf16[64,384]{1,0:T(8,128)(2,1)S(1)}, bf16[64,384]{1,0:T(8,128)(2,1)S(1)}, u32[]{:S(2)}, u32[]{:S(2)}) collective-permute-start(bf16[64,384]{1,0:T(8,128)(2,1)S(1)} %pad_maximum_fusion.17), channel_id=1, source_target_pairs={{0,2},{1,3},{2,0},{3,1},{4,6},{5,7},{6,4},{7,5},{8,10},{9,11},{10,... | collective-permute-start | bytes 147464 | tf_op jit(solution)/shard_map/ppermute | solution.py:29
  82.5 6.5 %collective-permute-start.24 = (bf16[64,384]{1,0:T(8,128)(2,1)S(1)}, bf16[64,384]{1,0:T(8,128)(2,1)S(1)}, u32[]{:S(2)}, u32[]{:S(2)}) collective-permute-start(bf16[64,384]{1,0:T(8,128)(2,1)S(1)} %pad_maximum_fusion.16), channel_id=1, source_target_pairs={{0,6},{1,7},{2,4},{3,5},{4,2},{5,3},{6,0},{7,1},{8,14},{9,15},{10,... | collective-permute-start | bytes 147464 | tf_op jit(solution)/shard_map/ppermute | solution.py:29
  85.1 5.0 %collective-permute-start.23 = (bf16[64,384]{1,0:T(8,128)(2,1)S(1)}, bf16[64,384]{1,0:T(8,128)(2,1)S(1)}, u32[]{:S(2)}, u32[]{:S(2)}) collective-permute-start(bf16[64,384]{1,0:T(8,128)(2,1)S(1)} %pad_maximum_fusion.16), channel_id=1, source_target_pairs={{0,4},{1,5},{2,6},{3,7},{4,0},{5,1},{6,2},{7,3},{8,12},{9,13},{10,... | collective-permute-start | bytes 147464 | tf_op jit(solution)/shard_map/ppermute | solution.py:29
  85.1 5.0 %collective-permute-start.22 = (bf16[64,384]{1,0:T(8,128)(2,1)S(1)}, bf16[64,384]{1,0:T(8,128)(2,1)S(1)}, u32[]{:S(2)}, u32[]{:S(2)}) collective-permute-start(bf16[64,384]{1,0:T(8,128)(2,1)S(1)} %pad_maximum_fusion.16), channel_id=1, source_target_pairs={{0,2},{1,3},{2,0},{3,1},{4,6},{5,7},{6,4},{7,5},{8,10},{9,11},{10,... | collective-permute-start | bytes 147464 | tf_op jit(solution)/shard_map/ppermute | solution.py:29
  102.4 5.7 %collective-permute-start.32 = (bf16[48,768]{1,0:T(8,128)(2,1)S(1)}, bf16[48,768]{1,0:T(8,128)(2,1)S(1)}, u32[]{:S(2)}, u32[]{:S(2)}) collective-permute-start(bf16[48,768]{1,0:T(8,128)(2,1)S(1)} %get-tuple-element.25), channel_id=1, source_target_pairs={{0,24},{8,16},{16,8},{24,0},{1,25},{9,17},{17,9},{25,1},{2,26},{10... | collective-permute-start | bytes 221192 | tf_op jit(solution)/shard_map/ppermute | solution.py:24
  104.1 5.6 %collective-permute-start.31 = (bf16[48,768]{1,0:T(8,128)(2,1)S(1)}, bf16[48,768]{1,0:T(8,128)(2,1)S(1)}, u32[]{:S(2)}, u32[]{:S(2)}) collective-permute-start(bf16[48,768]{1,0:T(8,128)(2,1)S(1)} %get-tuple-element.26), channel_id=1, source_target_pairs={{0,16},{8,24},{16,0},{24,8},{1,17},{9,25},{17,1},{25,9},{2,18},{10... | collective-permute-start | bytes 221192 | tf_op jit(solution)/shard_map/ppermute | solution.py:24
  104.6 5.1 %collective-permute-start.30 = (bf16[48,768]{1,0:T(8,128)(2,1)S(1)}, bf16[48,768]{1,0:T(8,128)(2,1)S(1)}, u32[]{:S(2)}, u32[]{:S(2)}) collective-permute-start(bf16[48,768]{1,0:T(8,128)(2,1)S(1)} %get-tuple-element.24), channel_id=1, source_target_pairs={{0,8},{8,0},{16,24},{24,16},{1,9},{9,1},{17,25},{25,17},{2,10},{10... | collective-permute-start | bytes 221192 | tf_op jit(solution)/shard_map/ppermute | solution.py:24
  (26 other events, 108.8 us)
where the time goes:
time: 111 us
  starting transfers between devices  36.9 us (33%)
  waiting for transfers between devices  26.6 us (24%)
  local copies, waits for them, and re-layouts  14.7 us (13%)
  other arithmetic  14.2 us (13%)
  matrix products  9.17 us (8%)
  Pallas kernels  7.92 us (7%)
  between operations  1.51 us (1%)
    ppermute x11, waiting for transfers between devices, over_text(): return lax.ppermute(array, 'text', [(i, i ^ step) for i in range(count)])  21.8 us
    ppermute x20, starting transfers between devices, over_graph(): return lax.ppermute(array, 'graph', [(i, i ^ step) for i in range(count)])  20.4 us
    ppermute x11, starting transfers between devices, over_text(): return lax.ppermute(array, 'text', [(i, i ^ step) for i in range(count)])  14.4 us
    dot_general x19, matrix products, dot(): lax.dot_general(left, right, (contract, batch), preferred_element_type=f32)  8.98 us
    unnamed x49, local copies, waits for them, and re-layouts  8.18 us
    pallas_call x1, Pallas kernels, attention(): pl.pallas_call(attention_kernel, out_shape=(pooled, pooled), in_specs=[vm...  7.92 us
    ppermute x20, waiting for transfers between devices, over_graph(): return lax.ppermute(array, 'graph', [(i, i ^ step) for i in range(count)])  4.83 us
    reduce_sum x1, other arithmetic, node_stage(): jnp.sum((listed[..., None] == extended_name).astype(f32), axis=2)  3.24 us
  transfers between devices with their start and end apart: 33, of which 8 were waited for; matrix products, arithmetic and copies ran while one was open for 20% of the time, Pallas kernels for 0%

commit v1 on v0

--- a/solution.py
+++ b/solution.py
@@ -1,3 +1,5 @@
+import functools
+
 import jax
 import jax.numpy as jnp
 from jax import lax
@@ -91,10 +93,19 @@
     return natural(parts, text).reshape(-1, parts[0].shape[1])
 
 
-def gather_graph(array):
+def fetch_graph(array):
     count = lax.axis_size("graph")
-    mine = jnp.stack([array] + [over_graph(array, k) for k in range(CORES, count, CORES)])
-    return jnp.stack([mine, over_graph(mine, 1)], axis=1).reshape((count,) + array.shape)
+    return [array] + [over_graph(array, k) for k in range(CORES, count, CORES)]
+
+
+def swap_cores(fetched):
+    mine = jnp.stack(fetched)
+    return mine, over_graph(mine, 1)
+
+
+def share_cores(fetched):
+    both = jnp.stack(swap_cores(fetched), axis=1)
+    return both.reshape((-1,) + fetched[0].shape)
 
 
 def layer_norm(tokens, in_gain, in_bias):
@@ -189,6 +200,180 @@
     )(normed, doc_ids, doc_ids.T, *pieces)
 
 
+def structure_kernel(mine, swapped, links, table, *, fan, slot_count, made):
+    texts, nodes, _ = links.shape
+    graphs = table.shape[0]
+    rows = nodes // graphs
+    lanes = texts * rows
+    capacity = rows // texts
+    text, graph = lax.axis_index("text"), lax.axis_index("graph")
+    facts = [(swapped if d % CORES else mine)[d // CORES].astype(f32) for d in range(graphs)]
+    tails = jnp.concatenate([each[fan : fan + 1] for each in facts]).astype(jnp.int32)
+    lane = lax.broadcasted_iota(jnp.int32, (graphs, lanes), 1)
+
+    owner_at = graphs * slot_count
+    own = lane % rows - owner_at
+    earlier = jnp.zeros_like(tails)
+    for j in range(1, made):
+        earlier += jnp.where((own >= j) & (pltpu.roll(tails, j, 1) == tails), 1, 0)
+    place = (tails ^ text) * rows + (text ^ (lane // rows)) * capacity + earlier
+    place = jnp.concatenate(
+        [place[:, t * rows + owner_at : t * rows + owner_at + made] for t in range(texts)], axis=1
+    )
+    row = lax.broadcasted_iota(jnp.int32, (lanes, texts * made), 0)
+    for d in range(graphs):
+        table[d] = jnp.where(row == place[d : d + 1], 1.0, 0.0).astype(bf16)
+
+    turned = tails
+    bit = 1
+    while bit < graphs:
+        step = bit * slot_count
+        up, down = pltpu.roll(turned, step, 1), pltpu.roll(turned, lanes - step, 1)
+        moved = jnp.where((lane // slot_count) & bit != 0, up, down)
+        turned = jnp.where(graph & bit != 0, moved, turned)
+        bit *= 2
+    entry = lax.broadcasted_iota(jnp.int32, (rows + owner_at, lanes), 0)
+    outer = entry - rows
+    name = rows + (graph ^ (outer % graphs)) * slot_count + outer // graphs
+    name = jnp.where(entry < rows, entry, name).astype(f32)
+    column = lax.broadcasted_iota(jnp.int32, (rows, nodes), 1)
+    inner = lax.broadcasted_iota(jnp.int32, (rows, nodes), 0)
+    base = lax.broadcasted_iota(jnp.int32, (graphs, nodes), 0) * rows
+    for d in range(graphs):
+        counts = jnp.zeros((rows + owner_at, lanes), f32)
+        for f in range(fan):
+            counts += jnp.where(facts[d][f : f + 1] == name, 1.0, 0.0)
+        counts = counts.T.astype(bf16)
+        for t in range(texts):
+            spots = [jnp.where(column == inner + d * rows, 1.0, 0.0)]
+            for k in range(slot_count):
+                at = t * rows + d * slot_count + k
+                target = base + turned[:, at : at + 1]
+                spots.append(jnp.where(column[:graphs] == target, 1.0, 0.0))
+            spots = jnp.concatenate(spots).astype(bf16)
+            linked = dot(counts[t * rows : (t + 1) * rows], spots, ((1,), (0,)))
+            links[t, d * rows : (d + 1) * rows, :] = linked.astype(bf16)
+
+
+def node_kernel(mine, swapped, up_mine, up_swapped, table, links, one, two, out, own, live_out, *refs, fan):
+    first_self, first_next, up_self, up_next, live, kept = refs
+    texts, nodes, _ = links.shape
+    graphs = table.shape[0]
+    rows = nodes // graphs
+    made = table.shape[2] // texts
+    hidden = two.shape[1]
+    ones = jnp.ones((texts * made, live.shape[2]), bf16)
+    for d in range(graphs):
+        chosen = table[d]
+        values = (swapped if d % CORES else mine)[d // CORES]
+        ups = (up_swapped if d % CORES else up_mine)[d // CORES]
+        for target, value in (
+            (live, ones),
+            (first_self, values[:, :hidden]),
+            (first_next, values[:, hidden:]),
+            (up_self, ups[:, :hidden]),
+            (up_next, ups[:, hidden:]),
+        ):
+            placed = dot(chosen, value, ((1,), (0,))).astype(bf16)
+            for t in range(texts):
+                target[t, d * rows : (d + 1) * rows, :] = placed[t * rows : (t + 1) * rows]
+    for t in range(texts):
+        linked = links[t]
+        x = first_self[t].astype(f32) + dot(linked, first_next[t], ((1,), (0,))) / fan
+        into = up_self[t].astype(f32) + dot(linked, up_next[t], ((0,), (0,))) / fan
+        alive = live[t][:, :1].astype(f32)
+        square = x * x
+        slope = 0.7978845608028654 * (1.0 + 3.0 * 0.044715 * square)
+        half = 0.5 * (1.0 + jnp.tanh(0.7978845608028654 * (x + 0.044715 * square * x)))
+        value = (alive * (x * half)).astype(bf16)
+        grad = (alive * ((half + 2.0 * x * half * (1.0 - half) * slope) * into)).astype(bf16)
+        at = slice(t * rows, (t + 1) * rows)
+        kept[0, at, :] = value[:rows]
+        kept[1, at, :] = (dot(linked[:rows], value, ((1,), (0,))) / fan).astype(bf16)
+        kept[2, at, :] = grad[:rows]
+        kept[3, at, :] = (dot(linked[:, :rows], grad, ((0,), (0,))) / fan).astype(bf16)
+    state = dot(kept[0], two[0], ((1,), (0,))) + dot(kept[1], two[1], ((1,), (0,)))
+    back = [dot(table[0], kept[i], ((0,), (0,))).astype(bf16) for i in (2, 3)]
+    returned = dot(back[0], one[0], ((1,), (1,))) + dot(back[1], one[1], ((1,), (1,)))
+    for t in range(texts):
+        out[t, :rows, :] = state[t * rows : (t + 1) * rows].astype(bf16)
+        out[t, rows:, :] = returned[t * made : (t + 1) * made].astype(bf16)
+    own[:rows, :] = state[:rows]
+    own[rows:, :] = returned[:made]
+    live_out[...] = live[0, :rows, :].astype(f32)
+
+
+def unpack_kernel(mine, swapped, one, two, *, depth, share):
+    graph = lax.axis_index("graph")
+    graphs = CORES * mine.shape[0]
+    hidden, width = two.shape[1:]
+    lanes = mine.shape[2]
+    same = graph % CORES == 0
+    for g in range(graphs):
+        z = (graph // CORES) ^ (g // CORES)
+        near, far = mine[z], swapped[z]
+        got = jnp.where(same == (g % CORES == 0), near, far)
+        half, j = g // (graphs // 2), g % (graphs // 2)
+        one[half, j * depth : (j + 1) * depth, :] = got[:depth, :hidden]
+        for m in range(width // lanes):
+            part = got[depth + m * share : depth + (m + 1) * share]
+            two[half, j * share : (j + 1) * share, m * lanes : (m + 1) * lanes] = part
+
+
+def unpack(mine, swapped, depth, share, hidden, width):
+    vmem = pl.BlockSpec(memory_space=pltpu.VMEM)
+    return pl.pallas_call(
+        functools.partial(unpack_kernel, depth=depth, share=share),
+        out_shape=(
+            jax.ShapeDtypeStruct((2, width, hidden), bf16),
+            jax.ShapeDtypeStruct((2, hidden, width), bf16),
+        ),
+        in_specs=[vmem] * 2,
+        out_specs=(vmem, vmem),
+        cost_estimate=pl.CostEstimate(flops=10**8, bytes_accessed=10**6, transcendentals=0),
+        name="unpack",
+    )(mine, swapped)
+
+
+def structure(mine, swapped, texts, graphs, rows, **sizes):
+    vmem = pl.BlockSpec(memory_space=pltpu.VMEM)
+    nodes, made = graphs * rows, sizes["made"]
+    return pl.pallas_call(
+        functools.partial(structure_kernel, **sizes),
+        out_shape=(
+            jax.ShapeDtypeStruct((texts, nodes, nodes), bf16),
+            jax.ShapeDtypeStruct((graphs, texts * rows, texts * made), bf16),
+        ),
+        in_specs=[vmem] * 2,
+        out_specs=(vmem, vmem),
+        cost_estimate=pl.CostEstimate(flops=10**9, bytes_accessed=10**6, transcendentals=0),
+        name="structure",
+    )(mine, swapped)
+
+
+def node_stage_parts(arrays, fan):
+    vmem = pl.BlockSpec(memory_space=pltpu.VMEM)
+    table, links, _, two = arrays[4:]
+    texts, nodes, _ = links.shape
+    rows = nodes // table.shape[0]
+    made = table.shape[2] // texts
+    hidden, width = two.shape[1:]
+    return pl.pallas_call(
+        functools.partial(node_kernel, fan=fan),
+        out_shape=(
+            jax.ShapeDtypeStruct((texts, rows + made, width), bf16),
+            jax.ShapeDtypeStruct((rows + made, width), f32),
+            jax.ShapeDtypeStruct((rows, 128), f32),
+        ),
+        in_specs=[vmem] * len(arrays),
+        out_specs=(vmem,) * 3,
+        scratch_shapes=[pltpu.VMEM((texts, nodes, hidden), bf16)] * 4
+        + [pltpu.VMEM((texts, nodes, 128), bf16), pltpu.VMEM((4, texts * rows, hidden), bf16)],
+        cost_estimate=pl.CostEstimate(flops=10**9, bytes_accessed=10**6, transcendentals=10**6),
+        name="nodes",
+    )(*arrays)
+
+
 def local(
     tokens,
     doc_ids,
@@ -206,7 +391,7 @@
     width = tokens.shape[1]
     texts, graphs = lax.axis_size("text"), lax.axis_size("graph")
     text, graph = lax.axis_index("text"), lax.axis_index("graph")
-    core, z = graph % CORES, graph // CORES
+    core = graph % CORES
     rows = out_grad.shape[0]
     made = owner_text.shape[0]
     capacity = rows // texts
@@ -218,7 +403,6 @@
     qkv_fetched = fetch_text(qkv_shard, core)
     out_fetched = fetch_text(out_shard, core)
     qkv_pieces = pieces_of(qkv_shard, qkv_fetched)
-    out_pieces = pieces_of(out_shard, out_fetched)
 
     depth = sage_one.shape[0]
     share = depth // texts
@@ -233,26 +417,23 @@
     packed = jnp.concatenate(
         [one_share] + [two_share[:, i : i + lanes] for i in range(0, width, lanes)], axis=0
     )
-    got = gather_graph(packed)
-    got = natural(
-        [got[CORES * k : CORES * (k + 1)] for k in range(graphs // CORES)], z
-    )
-    got = jnp.where(core == 0, got, got[:, ::-1]).reshape(graphs, -1, lanes)
-    one = got[:, :depth].reshape(2, width, lanes)
-    two = got[:, depth:].reshape(2, hidden // share, width // lanes, share, lanes)
-    two = two.transpose(0, 1, 3, 2, 4).reshape(2, hidden, width)
-    one = one[:, :, :hidden]
-
-    facts = jnp.concatenate(
-        [neighbours.reshape(-1), boundary.reshape(-1), owner_text.reshape(-1)]
-    ).astype(bf16)
-    fact_count = facts.shape[0]
-    fact_rows = -(-fact_count // width)
-    facts = jnp.pad(facts, (0, fact_rows * width - fact_count)).reshape(fact_rows, width)
-    outset = jnp.concatenate([out_grad, facts], axis=0)
-    outset = jnp.stack([outset] + [over_text(outset, k) for k in range(1, texts)])
-    grads = outset[:, :rows]
-    facts = outset[:, rows:].reshape(texts, -1)[:, :fact_count]
+    sage_fetched = fetch_graph(packed)
+
+    tail = jnp.concatenate([boundary.reshape(-1), owner_text.reshape(-1)])
+    tail_count = tail.shape[0]
+    tail = jnp.pad(tail, (0, -tail_count % rows)).reshape(-1, rows)
+    facts = jnp.concatenate([neighbours.T, tail], axis=0).astype(bf16)
+    fact_rows = facts.shape[0]
+    facts = jnp.pad(facts, ((0, rows - fact_rows), (0, -rows % 128)))
+    outset = jnp.concatenate([out_grad, facts], axis=1)
+    outset = [outset] + [over_text(outset, k) for k in range(1, texts)]
+    grads = jnp.concatenate([part[:, :width] for part in outset], axis=0)
+    facts = jnp.concatenate([part[:fact_rows, width : width + rows] for part in outset], axis=1)
+
+    def tail_of(facts):
+        tail = facts[..., fan:, :].reshape(facts.shape[:-2] + (fact_rows - fan, texts, rows))
+        tail = jnp.moveaxis(tail, -2, -3).reshape(facts.shape[:-2] + (texts, -1))
+        return tail.astype(i32)
 
     def slot_places(owners):
         same = owners[..., :, None] == owners[..., None, :]
@@ -262,51 +443,75 @@
         place = (owners ^ text) * rows + source[:, None] * capacity + earlier
         return place.reshape(owners.shape[:-2] + (1, texts * made))
 
-    own_places = slot_places(facts[:, fact_count - made :].astype(i32))
+    own_places = slot_places(tail_of(facts)[:, tail_count - made : tail_count])
     own_table = (own_places == jnp.arange(texts * rows, dtype=i32)[:, None]).astype(bf16)
     wide = 2 * hidden
-    all_count = texts * fact_count
-    all_rows = -(-all_count // width)
-    flat = jnp.pad(facts.reshape(-1), (0, all_rows * width - all_count)).reshape(all_rows, width)
-    facts = gather_graph(flat).reshape(graphs, -1)[:, :all_count]
-    facts = facts.reshape(graphs, texts, fact_count).astype(i32)
-
-    listed = facts[..., : rows * fan].reshape(graphs, texts, rows, fan)
-    bounds = facts[..., rows * fan : fact_count - made].reshape(graphs, texts, graphs, slot_count)
-    owners = facts[..., fact_count - made :]
-    places = slot_places(owners)
-    peer = graph ^ jnp.arange(graphs, dtype=i32)
-    halo_name = (rows + peer[:, None] * slot_count + jnp.arange(slot_count, dtype=i32)).reshape(-1)
-    extended_name = jnp.concatenate([jnp.arange(rows, dtype=i32), halo_name])
-    turned = (jnp.arange(graphs, dtype=i32)[:, None] == peer[None, :]).astype(f32)
-    halo_row = jnp.einsum("ptgk,gd->tdpk", bounds.astype(f32), turned).astype(i32)
-    halo_row = halo_row.reshape(texts, graphs, graphs * slot_count)
-    halo_at = jnp.repeat(jnp.arange(graphs, dtype=i32), slot_count) * rows + halo_row
-    nodes = graphs * rows
-
-    def node_stage(one_text):
-        distance, listed, halo_at = one_text
-        counts = jnp.sum((listed[..., None] == extended_name).astype(f32), axis=2).astype(bf16)
-        table = (places == distance * rows + jnp.arange(rows, dtype=i32)[:, None]).astype(bf16)
-        live = jnp.sum(table.astype(f32), axis=2).reshape(nodes, 1)
-
-        def to_rows(by_abstract):
-            return dot(table, by_abstract, ((2,), (1,)), ((0,), (0,))).reshape(nodes, -1)
-
-        if dense:
-            self_at = jnp.arange(nodes, dtype=i32).reshape(graphs, rows)
-            at = jnp.concatenate([self_at, halo_at], axis=1)
-            place = (at[..., None] == jnp.arange(nodes, dtype=i32)).astype(bf16)
-            links = dot(counts, place, ((2,), (1,)), ((0,), (0,)))
-            links = links.astype(bf16).reshape(nodes, nodes)
-
-            def pull(values, count):
-                return dot(links[:count], values, ((1,), (0,)))
-
-            def push(values, count):
-                return dot(links[:, :count], values, ((0,), (0,)))
-
-        else:
+    facts_fetched = fetch_graph(facts)
+
+    one, two = unpack(*swap_cores(sage_fetched), depth, share, hidden, width)
+    normed = layer_norm(tokens, in_gain, in_bias)
+    pooled_norm, pooled_context = attention(normed, doc_ids, qkv_pieces)
+    out_fetched, facts_fetched, pooled_context = lax.optimization_barrier(
+        (out_fetched, facts_fetched, pooled_context)
+    )
+    out_pieces = pieces_of(out_shard, out_fetched)
+    out_proj = assemble(out_pieces, text, core)
+    embedded = dot(pooled_context.astype(bf16), out_proj, ((1,), (1,)))
+    embedded = (pooled_norm + embedded).astype(bf16)
+    grads, embedded = lax.optimization_barrier((grads, embedded))
+    live_grad = dot(own_table, grads, ((0,), (0,))).astype(bf16)
+    up = jnp.concatenate(
+        [dot(live_grad, two[0], ((1,), (1,))), dot(live_grad, two[1], ((1,), (1,)))], axis=1
+    ).astype(bf16)
+    up_fetched = fetch_graph(up)
+    gathered = jnp.concatenate(
+        [embedded] + [over_text(embedded, k) for k in range(1, texts)], axis=0
+    )
+    first = jnp.concatenate(
+        [dot(gathered, one[0], ((1,), (0,))), dot(gathered, one[1], ((1,), (0,)))], axis=1
+    ).astype(bf16)
+    first_fetched = fetch_graph(first)
+
+    if texts * rows == 128 and tail_count == rows and capacity * texts == rows:
+        links, table = structure(
+            *swap_cores(facts_fetched),
+            texts,
+            graphs,
+            rows,
+            fan=fan,
+            slot_count=slot_count,
+            made=made,
+        )
+        parts = (*swap_cores(first_fetched), *swap_cores(up_fetched))
+        outgoing, total, live = node_stage_parts((*parts, table, links, one, two), fan)
+        live = live[:, :1]
+    else:
+        facts = share_cores(facts_fetched)
+        ups = share_cores(up_fetched)
+        firsts = share_cores(first_fetched)
+        listed = facts[:, :fan].reshape(graphs, fan, texts, rows).transpose(0, 2, 3, 1).astype(i32)
+        tail = tail_of(facts)
+        bounds = tail[..., : tail_count - made].reshape(graphs, texts, graphs, slot_count)
+        owners = tail[..., tail_count - made : tail_count]
+        places = slot_places(owners)
+        peer = graph ^ jnp.arange(graphs, dtype=i32)
+        halo_name = (rows + peer[:, None] * slot_count + jnp.arange(slot_count, dtype=i32)).reshape(-1)
+        extended_name = jnp.concatenate([jnp.arange(rows, dtype=i32), halo_name])
+        turned = (jnp.arange(graphs, dtype=i32)[:, None] == peer[None, :]).astype(f32)
+        halo_row = jnp.einsum("ptgk,gd->tdpk", bounds.astype(f32), turned).astype(i32)
+        halo_row = halo_row.reshape(texts, graphs, graphs * slot_count)
+        halo_at = jnp.repeat(jnp.arange(graphs, dtype=i32), slot_count) * rows + halo_row
+        nodes = graphs * rows
+
+        def node_stage(one_text):
+            distance, listed, halo_at = one_text
+            counts = jnp.sum((listed[..., None] == extended_name).astype(f32), axis=2).astype(bf16)
+            table = (places == distance * rows + jnp.arange(rows, dtype=i32)[:, None]).astype(bf16)
+            live = jnp.sum(table.astype(f32), axis=2).reshape(nodes, 1)
+
+            def to_rows(by_abstract):
+                return dot(table, by_abstract, ((2,), (1,)), ((0,), (0,))).reshape(nodes, -1)
+
             halo = halo_at.reshape(-1)
 
             def pull(values, count):
@@ -321,63 +526,39 @@
                 inner = out[:, :rows].reshape(nodes, -1)
                 return inner.at[halo].add(out[:, rows:].reshape(halo.shape[0], -1))[:count]
 
-        up_rows = to_rows(ups)
-        into_one = up_rows[:, :hidden] + push(up_rows[:, hidden:].astype(bf16), nodes) / fan
-        first_rows = to_rows(firsts)
-        preact_one = first_rows[:, :hidden] + pull(first_rows[:, hidden:].astype(bf16), nodes) / fan
-        gelu_value, pull_back = jax.vjp(jax.nn.gelu, preact_one)
-        hidden_one = (live * gelu_value).astype(bf16)
-        grad_one = (live * pull_back(into_one)[0]).astype(bf16)
-        aggregated = (pull(hidden_one, rows) / fan).astype(bf16)
-        returned = (push(grad_one, rows) / fan).astype(bf16)
-        return (
-            jnp.concatenate([hidden_one[:rows], aggregated], axis=1),
-            jnp.concatenate([grad_one[:rows], returned], axis=1),
-            live[:rows],
+            up_rows = to_rows(ups)
+            into_one = up_rows[:, :hidden] + push(up_rows[:, hidden:].astype(bf16), nodes) / fan
+            first_rows = to_rows(firsts)
+            preact_one = first_rows[:, :hidden] + pull(first_rows[:, hidden:].astype(bf16), nodes) / fan
+            gelu_value, pull_back = jax.vjp(jax.nn.gelu, preact_one)
+            hidden_one = (live * gelu_value).astype(bf16)
+            grad_one = (live * pull_back(into_one)[0]).astype(bf16)
+            aggregated = (pull(hidden_one, rows) / fan).astype(bf16)
+            returned = (push(grad_one, rows) / fan).astype(bf16)
+            return (
+                jnp.concatenate([hidden_one[:rows], aggregated], axis=1),
+                jnp.concatenate([grad_one[:rows], returned], axis=1),
+                live[:rows],
+            )
+
+        per_text = (jnp.arange(texts, dtype=i32), listed.transpose(1, 0, 2, 3), halo_at)
+        forth, back, live = lax.map(node_stage, per_text)
+        forth = forth.reshape(texts * rows, wide)
+        state_part = dot(forth[:, :hidden], two[0], ((1,), (0,))) + dot(
+            forth[:, hidden:], two[1], ((1,), (0,))
         )
-
-    normed = layer_norm(tokens, in_gain, in_bias)
-    pooled_norm, pooled_context = attention(normed, doc_ids, qkv_pieces)
-    out_proj = assemble(out_pieces, text, core)
-    embedded = dot(pooled_context.astype(bf16), out_proj, ((1,), (1,)))
-    embedded = (pooled_norm + embedded).astype(bf16)
-    grads, embedded = lax.optimization_barrier((grads, embedded))
-    live_grad = dot(own_table, grads.reshape(texts * rows, width), ((0,), (0,))).astype(bf16)
-    up = jnp.concatenate(
-        [dot(live_grad, two[0], ((1,), (1,))), dot(live_grad, two[1], ((1,), (1,)))], axis=1
-    ).astype(bf16)
-    ups = gather_graph(up)
-    gathered = jnp.concatenate(
-        [embedded] + [over_text(embedded, k) for k in range(1, texts)], axis=0
-    )
-    first = jnp.concatenate(
-        [dot(gathered, one[0], ((1,), (0,))), dot(gathered, one[1], ((1,), (0,)))], axis=1
-    ).astype(bf16)
-    firsts = gather_graph(first)
-
-    dense = texts * graphs <= 64
-    per_text = (jnp.arange(texts, dtype=i32), listed.transpose(1, 0, 2, 3), halo_at)
-    if dense:
-        forth, back, live = jax.vmap(node_stage)(per_text)
-    else:
-        forth, back, live = lax.map(node_stage, per_text)
-    forth = forth.reshape(texts * rows, wide)
-    state_part = dot(forth[:, :hidden], two[0], ((1,), (0,))) + dot(
-        forth[:, hidden:], two[1], ((1,), (0,))
-    )
-    back = dot(own_table, back.reshape(texts * rows, wide), ((0,), (0,))).astype(bf16)
-    grad_part = dot(back[:, :hidden], one[0], ((1,), (1,))) + dot(
-        back[:, hidden:], one[1], ((1,), (1,))
-    )
-
-    final = jnp.concatenate(
-        [state_part.reshape(texts, rows, width), grad_part.reshape(texts, made, width)], axis=1
-    )
-    total = final[0]
-    outgoing = final.astype(bf16)
+        back = dot(own_table, back.reshape(texts * rows, wide), ((0,), (0,))).astype(bf16)
+        grad_part = dot(back[:, :hidden], one[0], ((1,), (1,))) + dot(
+            back[:, hidden:], one[1], ((1,), (1,))
+        )
+
+        final = jnp.concatenate(
+            [state_part.reshape(texts, rows, width), grad_part.reshape(texts, made, width)], axis=1
+        )
+        total, outgoing, live = final[0], final.astype(bf16), live[0]
     for k in range(1, texts):
         total = total + over_text(outgoing[k], k).astype(f32)
-    node_states = (live[0] * total[:rows]).astype(bf16)
+    node_states = (live * total[:rows]).astype(bf16)
     return (node_states, total[rows:].astype(bf16))
 
 

time: 111 us -> 117 us (1.054)
  waiting for transfers between devices: 26.6 us -> 42.7 us
  Pallas kernels: 7.92 us -> 18.2 us
  matrix products: 9.17 us -> 1.74 us
  other arithmetic: 14.2 us -> 7.85 us
  local copies, waits for them, and re-layouts: 14.7 us -> 8.4 us
    ppermute x20, waiting for transfers between devices: 4.83 us -> 19.9 us  [over_graph(): return lax.ppermute(array, 'graph', [(i, i ^ step) for i in range(count)])]
    ppermute x2, waiting for transfers between devices: 0.01 us -> 14.9 us  [over_pair(): return lax.ppermute(array, ('text', 'graph'), moves)]
    ppermute x11, waiting for transfers between devices: 21.8 us -> 7.95 us  [over_text(): return lax.ppermute(array, 'text', [(i, i ^ step) for i in range(count)])]
    pallas_call x0 -> x3, Pallas kernels: none -> 10.2 us  [the longest x1 5.35 us: node_stage_parts(): pl.pallas_call(functools.partial(node_kernel, fan=fan), out_shape=(jax.Sh...]
    dot_general x19 -> x7, matrix products: 8.98 us -> 1.74 us  [dot(): lax.dot_general(left, right, (contract, batch), preferred_element_type=f32)]
    unnamed x49 -> x44, local copies, waits for them, and re-layouts: 8.18 us -> 3.63 us
    reduce_sum x2 -> x0, other arithmetic: 3.54 us -> none  [the longest x1 3.24 us: node_stage(): jnp.sum((listed[..., None] == extended_name).astype(f32), axis=2)]
    ppermute x20, starting transfers between devices: 20.4 us -> 17.9 us  [over_graph(): return lax.ppermute(array, 'graph', [(i, i ^ step) for i in range(count)])]
  transfers between devices with their start and end apart: 33 -> 33, of which waited for: 8 -> 14; matrix products, arithmetic and copies ran while one was open for 20% -> 6% of each run, Pallas kernels for 0% -> 11%
where the time goes in v1:
time: 117 us; the launch traced here: 116 us
  waiting for transfers between devices  42.7 us (36%)
  starting transfers between devices  36.1 us (31%)
  Pallas kernels  18.2 us (16%)
  local copies, waits for them, and re-layouts  8.4 us (7%)
  other arithmetic  7.85 us (7%)
  matrix products  1.74 us (1%)
  between operations  1.2 us (1%)
    ppermute x20, waiting for transfers between devices, over_graph(): return lax.ppermute(array, 'graph', [(i, i ^ step) for i in range(count)])  19.9 us
    ppermute x20, starting transfers between devices, over_graph(): return lax.ppermute(array, 'graph', [(i, i ^ step) for i in range(count)])  17.9 us
    ppermute x11, starting transfers between devices, over_text(): return lax.ppermute(array, 'text', [(i, i ^ step) for i in range(count)])  16 us
    ppermute x2, waiting for transfers between devices, over_pair(): return lax.ppermute(array, ('text', 'graph'), moves)  14.9 us
    ppermute x11, waiting for transfers between devices, over_text(): return lax.ppermute(array, 'text', [(i, i ^ step) for i in range(count)])  7.95 us
    pallas_call x1, Pallas kernels, attention(): pl.pallas_call(attention_kernel, out_shape=(pooled, pooled), in_specs=[vm...  7.93 us
    pallas_call x1, Pallas kernels, node_stage_parts(): pl.pallas_call(functools.partial(node_kernel, fan=fan), out_shape=(jax.Sh...  5.35 us
    unnamed x44, local copies, waits for them, and re-layouts  3.63 us
  transfers between devices with their start and end apart: 33, of which 14 were waited for; matrix products, arithmetic and copies ran while one was open for 6% of the time, Pallas kernels for 11%

profile of v1, /device:TPU:0, one launch (start us, length us, event | category | flops | bytes accessed | tf_op | source)
XLA Modules:
  0.0 116.2 jit_solution(12308155187842128690)
XLA Ops:
  3.9 3.0 %collective-permute-start = (bf16[32,896]{1,0:T(8,128)(2,1)S(1)}, bf16[32,896]{1,0:T(8,128)(2,1)S(1)}, u32[]{:S(2)}, u32[]{:S(2)}) collective-permute-start(bf16[32,896]{1,0:T(8,128)(2,1)S(1)} %pad_maximum_fusion.7), channel_id=1, source_target_pairs={{0,8},{8,0},{16,24},{24,16},{1,9},{9,1},{17,25},{25,17},{2,10},{10... | collective-permute-start | bytes 172040 | tf_op jit(solution)/shard_map/ppermute | solution.py:26
  6.8 1.5 %collective-permute-start.1 = (bf16[32,896]{1,0:T(8,128)(2,1)S(1)}, bf16[32,896]{1,0:T(8,128)(2,1)S(1)}, u32[]{:S(2)}, u32[]{:S(2)}) collective-permute-start(bf16[32,896]{1,0:T(8,128)(2,1)S(1)} %pad_maximum_fusion.7), channel_id=1, source_target_pairs={{0,16},{8,24},{16,0},{24,8},{1,17},{9,25},{17,1},{25,9},{2,18},{10... | collective-permute-start | bytes 172040 | tf_op jit(solution)/shard_map/ppermute | solution.py:26
  9.4 3.0 %collective-permute-start.5 = (bf16[576,384]{1,0:T(8,128)(2,1)S(1)}, bf16[576,384]{1,0:T(8,128)(2,1)}, u32[]{:S(2)}, u32[]{:S(2)}) collective-permute-start(bf16[576,384]{1,0:T(8,128)(2,1)S(1)} %dynamic-slice_bitcast_fusion), channel_id=1, source_target_pairs={{0,24},{8,16},{16,8},{24,0},{1,25},{9,17},{17,9},{25,1},{2,26},{10... | collective-permute-start | bytes 1327112 | tf_op jit(solution)/shard_map/ppermute | solution.py:26
  16.8 14.8 %collective-permute-done.3.refs_4_ = bf16[576,768]{1,0:T(8,128)(2,1)} collective-permute-done((bf16[576,768]{1,0:T(8,128)(2,1)}, bf16[576,768]{1,0:T(8,128)(2,1)}, u32[]{:S(2)}, u32[]{:S(2)}) %collective-permute-start.3) | collective-permute-done | bytes 884768 | tf_op jit(solution)/shard_map/ppermute | solution.py:40
  31.8 1.8 %collective-permute-start.17 = (bf16[336,256]{1,0:T(8,128)(2,1)S(1)}, bf16[336,256]{1,0:T(8,128)(2,1)S(1)}, u32[]{:S(2)}, u32[]{:S(2)}) collective-permute-start(bf16[336,256]{1,0:T(8,128)(2,1)S(1)} %get-tuple-element.53), channel_id=1, source_target_pairs={{0,2},{1,3},{2,0},{3,1},{4,6},{5,7},{6,4},{7,5},{8,10},{9,11},{10,... | collective-permute-start | bytes 516104 | tf_op jit(solution)/shard_map/ppermute | solution.py:31
  33.6 2.6 %collective-permute-start.18 = (bf16[336,256]{1,0:T(8,128)(2,1)S(1)}, bf16[336,256]{1,0:T(8,128)(2,1)S(1)}, u32[]{:S(2)}, u32[]{:S(2)}) collective-permute-start(bf16[336,256]{1,0:T(8,128)(2,1)S(1)} %get-tuple-element.53), channel_id=1, source_target_pairs={{0,4},{1,5},{2,6},{3,7},{4,0},{5,1},{6,2},{7,3},{8,12},{9,13},{10,... | collective-permute-start | bytes 516104 | tf_op jit(solution)/shard_map/ppermute | solution.py:31
  36.5 5.2 %collective-permute-done.17 = bf16[336,256]{1,0:T(8,128)(2,1)S(1)} collective-permute-done((bf16[336,256]{1,0:T(8,128)(2,1)S(1)}, bf16[336,256]{1,0:T(8,128)(2,1)S(1)}, u32[]{:S(2)}, u32[]{:S(2)}) %collective-permute-start.17) | collective-permute-done | bytes 172064 | tf_op jit(solution)/shard_map/ppermute | solution.py:31
  41.6 1.6 %collective-permute-start.7 = (bf16[192,768]{1,0:T(8,128)(2,1)S(1)}, bf16[192,768]{1,0:T(8,128)(2,1)S(1)}, u32[]{:S(2)}, u32[]{:S(2)}) collective-permute-start(bf16[192,768]{1,0:T(8,128)(2,1)S(1)} %bitcast.69), channel_id=1, source_target_pairs={{0,8},{1,17},{2,10},{3,19},{4,12},{5,21},{6,14},{7,23},{8,0},{9,25... | collective-permute-start | bytes 884744 | tf_op jit(solution)/shard_map/ppermute | solution.py:40
  43.2 5.9 %collective-permute-done.18 = bf16[336,256]{1,0:T(8,128)(2,1)S(1)} collective-permute-done((bf16[336,256]{1,0:T(8,128)(2,1)S(1)}, bf16[336,256]{1,0:T(8,128)(2,1)S(1)}, u32[]{:S(2)}, u32[]{:S(2)}) %collective-permute-start.18) | collective-permute-done | bytes 172064 | tf_op jit(solution)/shard_map/ppermute | solution.py:31
  50.1 3.5 %collective-permute-done.10 = bf16[16,128]{1,0:T(8,128)(2,1)S(1)} collective-permute-done((bf16[16,128]{1,0:T(8,128)(2,1)S(1)}, bf16[16,128]{1,0:T(8,128)(2,1)S(1)}, u32[]{:S(2)}, u32[]{:S(2)}) %collective-permute-start.10) | collective-permute-done | bytes 4128 | tf_op jit(solution)/shard_map/ppermute | solution.py:31
  55.1 2.5 %collective-permute-start.11 = (bf16[16,128]{1,0:T(8,128)(2,1)S(1)}, bf16[16,128]{1,0:T(8,128)(2,1)S(1)}, u32[]{:S(2)}, u32[]{:S(2)}) collective-permute-start(bf16[16,128]{1,0:T(8,128)(2,1)S(1)} %pad_maximum_fusion.11), channel_id=1, source_target_pairs={{0,6},{1,7},{2,4},{3,5},{4,2},{5,3},{6,0},{7,1},{8,14},{9,15},{10,... | collective-permute-start | bytes 12296 | tf_op jit(solution)/shard_map/ppermute | solution.py:31
  57.6 7.9 %attention.1 = (f32[16,768]{1,0:T(8,128)}, f32[16,768]{1,0:T(8,128)}) custom-call(bf16[512,768]{1,0:T(8,128)(2,1)} %fusion.5.refs_0_, s32[4,128]{1,0:T(4,128)} %refs_1_.1, s32[128,4]{1,0:T(8,128)} %bitcast.80, bf16[576,768]{1,0:T(8,128)(2,1)} %bitcast.72, bf16[576,768]{1,0:T(8,128)(2,1)} %collective-permute-done.3.refs_4_, ...), custom_call_target="tpu_custom_call" | custom-call | flops 2113929216 | bytes 4718592 | tf_op jit(solution)/shard_map/attention/pallas_call | solution.py:185
  66.8 2.5 %unpack.1 = (bf16[2,768,192]{2,1,0:T(8,128)(2,1)}, bf16[2,192,768]{2,1,0:T(8,128)(2,1)}) custom-call(bf16[4,336,256]{2,1,0:T(8,128)(2,1)} %copy-done.2, bf16[4,336,256]{2,1,0:T(8,128)(2,1)} %copy-done.3), custom_call_target="tpu_custom_call" | custom-call | flops 100000000 | bytes 1000000 | tf_op jit(solution)/shard_map/unpack/pallas_call | solution.py:325
  73.3 2.1 %collective-permute-start.25 = (bf16[64,384]{1,0:T(8,128)(2,1)S(1)}, bf16[64,384]{1,0:T(8,128)(2,1)S(1)}, u32[]{:S(2)}, u32[]{:S(2)}) collective-permute-start(bf16[64,384]{1,0:T(8,128)(2,1)S(1)} %pad_maximum_fusion.9), channel_id=1, source_target_pairs={{0,2},{1,3},{2,0},{3,1},{4,6},{5,7},{6,4},{7,5},{8,10},{9,11},{10,... | collective-permute-start | bytes 147464 | tf_op jit(solution)/shard_map/ppermute | solution.py:31
  75.4 2.4 %collective-permute-start.27 = (bf16[64,384]{1,0:T(8,128)(2,1)S(1)}, bf16[64,384]{1,0:T(8,128)(2,1)S(1)}, u32[]{:S(2)}, u32[]{:S(2)}) collective-permute-start(bf16[64,384]{1,0:T(8,128)(2,1)S(1)} %pad_maximum_fusion.9), channel_id=1, source_target_pairs={{0,6},{1,7},{2,4},{3,5},{4,2},{5,3},{6,0},{7,1},{8,14},{9,15},{10,... | collective-permute-start | bytes 147464 | tf_op jit(solution)/shard_map/ppermute | solution.py:31
  79.9 1.7 %collective-permute-done.14 = bf16[16,768]{1,0:T(8,128)(2,1)S(1)} collective-permute-done((bf16[16,768]{1,0:T(8,128)(2,1)S(1)}, bf16[16,768]{1,0:T(8,128)(2,1)S(1)}, u32[]{:S(2)}, u32[]{:S(2)}) %collective-permute-start.14) | collective-permute-done | bytes 24608 | tf_op jit(solution)/shard_map/ppermute | solution.py:26
  81.7 1.5 %collective-permute-start.16 = (bf16[16,768]{1,0:T(8,128)(2,1)S(1)}, bf16[16,768]{1,0:T(8,128)(2,1)S(1)}, u32[]{:S(2)}, u32[]{:S(2)}) collective-permute-start(bf16[16,768]{1,0:T(8,128)(2,1)S(1)} %add_convert_fusion), channel_id=1, source_target_pairs={{0,24},{8,16},{16,8},{24,0},{1,25},{9,17},{17,9},{25,1},{2,26},{10... | collective-permute-start | bytes 73736 | tf_op jit(solution)/shard_map/ppermute | solution.py:26
  83.2 3.2 %collective-permute-done.16 = bf16[16,768]{1,0:T(8,128)(2,1)S(1)} collective-permute-done((bf16[16,768]{1,0:T(8,128)(2,1)S(1)}, bf16[16,768]{1,0:T(8,128)(2,1)S(1)}, u32[]{:S(2)}, u32[]{:S(2)}) %collective-permute-start.16) | collective-permute-done | bytes 24608 | tf_op jit(solution)/shard_map/ppermute | solution.py:26
  88.9 2.4 %collective-permute-start.23 = (bf16[64,384]{1,0:T(8,128)(2,1)S(1)}, bf16[64,384]{1,0:T(8,128)(2,1)S(1)}, u32[]{:S(2)}, u32[]{:S(2)}) collective-permute-start(bf16[64,384]{1,0:T(8,128)(2,1)S(1)} %pad_maximum_fusion.8), channel_id=1, source_target_pairs={{0,6},{1,7},{2,4},{3,5},{4,2},{5,3},{6,0},{7,1},{8,14},{9,15},{10,... | collective-permute-start | bytes 147464 | tf_op jit(solution)/shard_map/ppermute | solution.py:31
  91.5 1.9 %collective-permute-done.22 = bf16[64,384]{1,0:T(8,128)(2,1)S(1)} collective-permute-done((bf16[64,384]{1,0:T(8,128)(2,1)S(1)}, bf16[64,384]{1,0:T(8,128)(2,1)S(1)}, u32[]{:S(2)}, u32[]{:S(2)}) %collective-permute-start.22) | collective-permute-done | bytes 49184 | tf_op jit(solution)/shard_map/ppermute | solution.py:31
  97.0 2.4 %structure.1 = (bf16[4,256,256]{2,1,0:T(8,128)(2,1)}, bf16[8,128,64]{2,1,0:T(8,128)(2,1)}) custom-call(bf16[4,16,128]{2,1,0:T(8,128)(2,1)} %copy-done.10, bf16[4,16,128]{2,1,0:T(8,128)(2,1)} %copy-done.19), custom_call_target="tpu_custom_call" | custom-call | flops 1000000000 | bytes 1000000 | tf_op jit(solution)/shard_map/structure/pallas_call | solution.py:341
  100.2 5.4 %nodes.1 = (bf16[4,48,768]{2,1,0:T(8,128)(2,1)}, f32[48,768]{1,0:T(8,128)}, f32[32,128]{1,0:T(8,128)}) custom-call(bf16[4,64,384]{2,1,0:T(8,128)(2,1)} %copy-done.7, bf16[4,64,384]{2,1,0:T(8,128)(2,1)} %copy-done.18, bf16[4,64,384]{2,1,0:T(8,128)(2,1)} %copy-done.6, bf16[4,64,384]{2,1,0:T(8,128)(2,1)} %copy-done.17, ...), custom_call_target="tpu_custom_call" | custom-call | flops 1000000000 | bytes 1000000 | tf_op jit(solution)/shard_map/nodes/pallas_call | solution.py:361
  108.6 1.4 %collective-permute-start.32 = (bf16[48,768]{1,0:T(8,128)(2,1)S(1)}, bf16[48,768]{1,0:T(8,128)(2,1)S(1)}, u32[]{:S(2)}, u32[]{:S(2)}) collective-permute-start(bf16[48,768]{1,0:T(8,128)(2,1)S(1)} %get-tuple-element.45), channel_id=1, source_target_pairs={{0,24},{8,16},{16,8},{24,0},{1,25},{9,17},{17,9},{25,1},{2,26},{10... | collective-permute-start | bytes 221192 | tf_op jit(solution)/shard_map/ppermute | solution.py:26
  111.9 2.0 %collective-permute-done.32 = bf16[48,768]{1,0:T(8,128)(2,1)S(1)} collective-permute-done((bf16[48,768]{1,0:T(8,128)(2,1)S(1)}, bf16[48,768]{1,0:T(8,128)(2,1)S(1)}, u32[]{:S(2)}, u32[]{:S(2)}) %collective-permute-start.32) | collective-permute-done | bytes 73760 | tf_op jit(solution)/shard_map/ppermute | solution.py:26
  (150 shorter events, 32.6 us)
Async XLA Ops:
  3.9 27.9 %collective-permute-start = (bf16[32,896]{1,0:T(8,128)(2,1)S(1)}, bf16[32,896]{1,0:T(8,128)(2,1)S(1)}, u32[]{:S(2)}, u32[]{:S(2)}) collective-permute-start(bf16[32,896]{1,0:T(8,128)(2,1)S(1)} %pad_maximum_fusion.7), channel_id=1, source_target_pairs={{0,8},{8,0},{16,24},{24,16},{1,9},{9,1},{17,25},{25,17},{2,10},{10... | collective-permute-start | bytes 172040 | tf_op jit(solution)/shard_map/ppermute | solution.py:26
  6.8 26.8 %collective-permute-start.1 = (bf16[32,896]{1,0:T(8,128)(2,1)S(1)}, bf16[32,896]{1,0:T(8,128)(2,1)S(1)}, u32[]{:S(2)}, u32[]{:S(2)}) collective-permute-start(bf16[32,896]{1,0:T(8,128)(2,1)S(1)} %pad_maximum_fusion.7), channel_id=1, source_target_pairs={{0,16},{8,24},{16,0},{24,8},{1,17},{9,25},{17,1},{25,9},{2,18},{10... | collective-permute-start | bytes 172040 | tf_op jit(solution)/shard_map/ppermute | solution.py:26
  8.4 27.9 %collective-permute-start.2 = (bf16[32,896]{1,0:T(8,128)(2,1)S(1)}, bf16[32,896]{1,0:T(8,128)(2,1)S(1)}, u32[]{:S(2)}, u32[]{:S(2)}) collective-permute-start(bf16[32,896]{1,0:T(8,128)(2,1)S(1)} %pad_maximum_fusion.7), channel_id=1, source_target_pairs={{0,24},{8,16},{16,8},{24,0},{1,25},{9,17},{17,9},{25,1},{2,26},{10... | collective-permute-start | bytes 172040 | tf_op jit(solution)/shard_map/ppermute | solution.py:26
  9.4 39.7 %collective-permute-start.5 = (bf16[576,384]{1,0:T(8,128)(2,1)S(1)}, bf16[576,384]{1,0:T(8,128)(2,1)}, u32[]{:S(2)}, u32[]{:S(2)}) collective-permute-start(bf16[576,384]{1,0:T(8,128)(2,1)S(1)} %dynamic-slice_bitcast_fusion), channel_id=1, source_target_pairs={{0,24},{8,16},{16,8},{24,0},{1,25},{9,17},{17,9},{25,1},{2,26},{10... | collective-permute-start | bytes 1327112 | tf_op jit(solution)/shard_map/ppermute | solution.py:26
  12.4 19.2 %collective-permute-start.3 = (bf16[576,768]{1,0:T(8,128)(2,1)}, bf16[576,768]{1,0:T(8,128)(2,1)}, u32[]{:S(2)}, u32[]{:S(2)}) collective-permute-start(bf16[576,768]{1,0:T(8,128)(2,1)} %bitcast.71), channel_id=1, source_target_pairs={{0,8},{1,17},{2,10},{3,19},{4,12},{5,21},{6,14},{7,23},{8,0},{9,25... | collective-permute-start | bytes 2654216 | tf_op jit(solution)/shard_map/ppermute | solution.py:40
  31.6 25.9 %collective-permute-start.4 = (bf16[576,768]{1,0:T(8,128)(2,1)}, bf16[576,768]{1,0:T(8,128)(2,1)}, u32[]{:S(2)}, u32[]{:S(2)}) collective-permute-start(bf16[576,768]{1,0:T(8,128)(2,1)} %collective-permute-done.3.refs_4_), channel_id=1, source_target_pairs={{0,1},{1,0},{2,3},{3,2},{4,5},{5,4},{6,7},{7,6},{8,9},{9,8},{10,11... | collective-permute-start | bytes 2654216 | tf_op jit(solution)/shard_map/ppermute | solution.py:31
  31.8 9.8 %collective-permute-start.17 = (bf16[336,256]{1,0:T(8,128)(2,1)S(1)}, bf16[336,256]{1,0:T(8,128)(2,1)S(1)}, u32[]{:S(2)}, u32[]{:S(2)}) collective-permute-start(bf16[336,256]{1,0:T(8,128)(2,1)S(1)} %get-tuple-element.53), channel_id=1, source_target_pairs={{0,2},{1,3},{2,0},{3,1},{4,6},{5,7},{6,4},{7,5},{8,10},{9,11},{10,... | collective-permute-start | bytes 516104 | tf_op jit(solution)/shard_map/ppermute | solution.py:31
  33.6 15.5 %collective-permute-start.18 = (bf16[336,256]{1,0:T(8,128)(2,1)S(1)}, bf16[336,256]{1,0:T(8,128)(2,1)S(1)}, u32[]{:S(2)}, u32[]{:S(2)}) collective-permute-start(bf16[336,256]{1,0:T(8,128)(2,1)S(1)} %get-tuple-element.53), channel_id=1, source_target_pairs={{0,4},{1,5},{2,6},{3,7},{4,0},{5,1},{6,2},{7,3},{8,12},{9,13},{10,... | collective-permute-start | bytes 516104 | tf_op jit(solution)/shard_map/ppermute | solution.py:31
  36.2 12.9 %collective-permute-start.19 = (bf16[336,256]{1,0:T(8,128)(2,1)S(1)}, bf16[336,256]{1,0:T(8,128)(2,1)S(1)}, u32[]{:S(2)}, u32[]{:S(2)}) collective-permute-start(bf16[336,256]{1,0:T(8,128)(2,1)S(1)} %get-tuple-element.53), channel_id=1, source_target_pairs={{0,6},{1,7},{2,4},{3,5},{4,2},{5,3},{6,0},{7,1},{8,14},{9,15},{10,... | collective-permute-start | bytes 516104 | tf_op jit(solution)/shard_map/ppermute | solution.py:31
  41.6 24.0 %collective-permute-start.7 = (bf16[192,768]{1,0:T(8,128)(2,1)S(1)}, bf16[192,768]{1,0:T(8,128)(2,1)S(1)}, u32[]{:S(2)}, u32[]{:S(2)}) collective-permute-start(bf16[192,768]{1,0:T(8,128)(2,1)S(1)} %bitcast.69), channel_id=1, source_target_pairs={{0,8},{1,17},{2,10},{3,19},{4,12},{5,21},{6,14},{7,23},{8,0},{9,25... | collective-permute-start | bytes 884744 | tf_op jit(solution)/shard_map/ppermute | solution.py:40
  49.2 5.9 %collective-permute-start.6 = (bf16[576,384]{1,0:T(8,128)(2,1)}, bf16[576,384]{1,0:T(8,128)(2,1)S(1)}, u32[]{:S(2)}, u32[]{:S(2)}) collective-permute-start(bf16[576,384]{1,0:T(8,128)(2,1)} %collective-permute-done.5.refs_6_), channel_id=1, source_target_pairs={{0,1},{1,0},{2,3},{3,2},{4,5},{5,4},{6,7},{7,6},{8,9},{9,8},{10,11... | collective-permute-start | bytes 1327112 | tf_op jit(solution)/shard_map/ppermute | solution.py:31
  49.3 16.6 %collective-permute-start.20 = (bf16[4,336,256]{2,1,0:T(8,128)(2,1)S(1)}, bf16[4,336,256]{2,1,0:T(8,128)(2,1)S(1)}, u32[]{:S(2)}, u32[]{:S(2)}) collective-permute-start(bf16[4,336,256]{2,1,0:T(8,128)(2,1)S(1)} %pad_maximum_fusion.2.mine), channel_id=1, source_target_pairs={{0,1},{1,0},{2,3},{3,2},{4,5},{5,4},{6,7},{7,6},{8,9},{9,8},{10,11... | collective-permute-start | bytes 2064392 | tf_op jit(solution)/shard_map/ppermute | solution.py:31
  53.7 11.9 %collective-permute-start.8 = (bf16[192,384]{1,0:T(8,128)(2,1)S(1)}, bf16[192,384]{1,0:T(8,128)(2,1)S(1)}, u32[]{:S(2)}, u32[]{:S(2)}) collective-permute-start(bf16[192,384]{1,0:T(8,128)(2,1)S(1)} %dynamic-slice_bitcast_fusion.1), channel_id=1, source_target_pairs={{0,24},{8,16},{16,8},{24,0},{1,25},{9,17},{17,9},{25,1},{2,26},{10... | collective-permute-start | bytes 442376 | tf_op jit(solution)/shard_map/ppermute | solution.py:26
  55.1 10.5 %collective-permute-start.11 = (bf16[16,128]{1,0:T(8,128)(2,1)S(1)}, bf16[16,128]{1,0:T(8,128)(2,1)S(1)}, u32[]{:S(2)}, u32[]{:S(2)}) collective-permute-start(bf16[16,128]{1,0:T(8,128)(2,1)S(1)} %pad_maximum_fusion.11), channel_id=1, source_target_pairs={{0,6},{1,7},{2,4},{3,5},{4,2},{5,3},{6,0},{7,1},{8,14},{9,15},{10,... | collective-permute-start | bytes 12296 | tf_op jit(solution)/shard_map/ppermute | solution.py:31
  57.6 8.0 %collective-permute-start.9 = (bf16[16,128]{1,0:T(8,128)(2,1)S(1)}, bf16[16,128]{1,0:T(8,128)(2,1)S(1)}, u32[]{:S(2)}, u32[]{:S(2)}) collective-permute-start(bf16[16,128]{1,0:T(8,128)(2,1)S(1)} %pad_maximum_fusion.11), channel_id=1, source_target_pairs={{0,2},{1,3},{2,0},{3,1},{4,6},{5,7},{6,4},{7,5},{8,10},{9,11},{10,... | collective-permute-start | bytes 12296 | tf_op jit(solution)/shard_map/ppermute | solution.py:31
  73.3 15.6 %collective-permute-start.25 = (bf16[64,384]{1,0:T(8,128)(2,1)S(1)}, bf16[64,384]{1,0:T(8,128)(2,1)S(1)}, u32[]{:S(2)}, u32[]{:S(2)}) collective-permute-start(bf16[64,384]{1,0:T(8,128)(2,1)S(1)} %pad_maximum_fusion.9), channel_id=1, source_target_pairs={{0,2},{1,3},{2,0},{3,1},{4,6},{5,7},{6,4},{7,5},{8,10},{9,11},{10,... | collective-permute-start | bytes 147464 | tf_op jit(solution)/shard_map/ppermute | solution.py:31
  75.4 15.9 %collective-permute-start.26 = (bf16[64,384]{1,0:T(8,128)(2,1)S(1)}, bf16[64,384]{1,0:T(8,128)(2,1)S(1)}, u32[]{:S(2)}, u32[]{:S(2)}) collective-permute-start(bf16[64,384]{1,0:T(8,128)(2,1)S(1)} %pad_maximum_fusion.9), channel_id=1, source_target_pairs={{0,4},{1,5},{2,6},{3,7},{4,0},{5,1},{6,2},{7,3},{8,12},{9,13},{10,... | collective-permute-start | bytes 147464 | tf_op jit(solution)/shard_map/ppermute | solution.py:31
  75.4 15.9 %collective-permute-start.27 = (bf16[64,384]{1,0:T(8,128)(2,1)S(1)}, bf16[64,384]{1,0:T(8,128)(2,1)S(1)}, u32[]{:S(2)}, u32[]{:S(2)}) collective-permute-start(bf16[64,384]{1,0:T(8,128)(2,1)S(1)} %pad_maximum_fusion.9), channel_id=1, source_target_pairs={{0,6},{1,7},{2,4},{3,5},{4,2},{5,3},{6,0},{7,1},{8,14},{9,15},{10,... | collective-permute-start | bytes 147464 | tf_op jit(solution)/shard_map/ppermute | solution.py:31
  81.7 4.7 %collective-permute-start.16 = (bf16[16,768]{1,0:T(8,128)(2,1)S(1)}, bf16[16,768]{1,0:T(8,128)(2,1)S(1)}, u32[]{:S(2)}, u32[]{:S(2)}) collective-permute-start(bf16[16,768]{1,0:T(8,128)(2,1)S(1)} %add_convert_fusion), channel_id=1, source_target_pairs={{0,24},{8,16},{16,8},{24,0},{1,25},{9,17},{17,9},{25,1},{2,26},{10... | collective-permute-start | bytes 73736 | tf_op jit(solution)/shard_map/ppermute | solution.py:26
  86.9 4.7 %collective-permute-start.21 = (bf16[64,384]{1,0:T(8,128)(2,1)S(1)}, bf16[64,384]{1,0:T(8,128)(2,1)S(1)}, u32[]{:S(2)}, u32[]{:S(2)}) collective-permute-start(bf16[64,384]{1,0:T(8,128)(2,1)S(1)} %pad_maximum_fusion.8), channel_id=1, source_target_pairs={{0,2},{1,3},{2,0},{3,1},{4,6},{5,7},{6,4},{7,5},{8,10},{9,11},{10,... | collective-permute-start | bytes 147464 | tf_op jit(solution)/shard_map/ppermute | solution.py:31
  88.0 5.5 %collective-permute-start.22 = (bf16[64,384]{1,0:T(8,128)(2,1)S(1)}, bf16[64,384]{1,0:T(8,128)(2,1)S(1)}, u32[]{:S(2)}, u32[]{:S(2)}) collective-permute-start(bf16[64,384]{1,0:T(8,128)(2,1)S(1)} %pad_maximum_fusion.8), channel_id=1, source_target_pairs={{0,4},{1,5},{2,6},{3,7},{4,0},{5,1},{6,2},{7,3},{8,12},{9,13},{10,... | collective-permute-start | bytes 147464 | tf_op jit(solution)/shard_map/ppermute | solution.py:31
  88.9 5.9 %collective-permute-start.23 = (bf16[64,384]{1,0:T(8,128)(2,1)S(1)}, bf16[64,384]{1,0:T(8,128)(2,1)S(1)}, u32[]{:S(2)}, u32[]{:S(2)}) collective-permute-start(bf16[64,384]{1,0:T(8,128)(2,1)S(1)} %pad_maximum_fusion.8), channel_id=1, source_target_pairs={{0,6},{1,7},{2,4},{3,5},{4,2},{5,3},{6,0},{7,1},{8,14},{9,15},{10,... | collective-permute-start | bytes 147464 | tf_op jit(solution)/shard_map/ppermute | solution.py:31
  91.4 8.0 %collective-permute-start.28 = (bf16[4,64,384]{2,1,0:T(8,128)(2,1)S(1)}, bf16[4,64,384]{2,1,0:T(8,128)(2,1)S(1)}, u32[]{:S(2)}, u32[]{:S(2)}) collective-permute-start(bf16[4,64,384]{2,1,0:T(8,128)(2,1)S(1)} %pad_maximum_fusion.5.up_mine), channel_id=1, source_target_pairs={{0,1},{1,0},{2,3},{3,2},{4,5},{5,4},{6,7},{7,6},{8,9},{9,8},{10,11... | collective-permute-start | bytes 589832 | tf_op jit(solution)/shard_map/ppermute | solution.py:31
  108.6 5.3 %collective-permute-start.32 = (bf16[48,768]{1,0:T(8,128)(2,1)S(1)}, bf16[48,768]{1,0:T(8,128)(2,1)S(1)}, u32[]{:S(2)}, u32[]{:S(2)}) collective-permute-start(bf16[48,768]{1,0:T(8,128)(2,1)S(1)} %get-tuple-element.45), channel_id=1, source_target_pairs={{0,24},{8,16},{16,8},{24,0},{1,25},{9,17},{17,9},{25,1},{2,26},{10... | collective-permute-start | bytes 221192 | tf_op jit(solution)/shard_map/ppermute | solution.py:26
  (29 other events, 130.7 us)

commit v2 on v1

--- a/solution.py
+++ b/solution.py
@@ -56,7 +56,8 @@
 
 
 def pieces_of(shard, fetched):
-    return [shard] + [piece for got in fetched for piece in (got, over_graph(got, 1))]
+    swapped = [over_graph(got, 1) for got in fetched]
+    return [shard] + [piece for both in zip(fetched, swapped) for piece in both]
 
 
 def place_pieces(refs, whole, sem):
@@ -116,11 +117,42 @@
     return (centred * lax.rsqrt(variance + epsilon) * in_gain + in_bias).astype(bf16)
 
 
-def attention_kernel(*refs):
+def place_shares(mine, swapped, one, two, sem, depth):
+    graph = lax.axis_index("graph")
+    count, height, lanes = mine.shape
+    width = two.shape[2]
+    share = (height - depth) * lanes // width
+    per_half = CORES * count // 2
+    copies = []
+    for k in range(count):
+        for source, core in ((mine, graph % CORES), (swapped, 1 - graph % CORES)):
+            peer = ((graph // CORES) ^ k) * CORES + core
+            half, j = peer // per_half, peer % per_half
+            at = pl.ds(pl.multiple_of(j * depth, depth), depth)
+            moves = [(source.at[k, :depth, :], one.at[half, at, :])]
+            at = pl.ds(pl.multiple_of(j * share, share), share)
+            for m in range(width // lanes):
+                start = depth + m * share
+                part = source.at[k, start : start + share, :]
+                moves.append((part, two.at[half, at, m * lanes : (m + 1) * lanes]))
+            for source_at, target in moves:
+                copies.append(pltpu.make_async_copy(source_at, target, sem.at[len(copies)]))
+    return copies
+
+
+def attention_kernel(*refs, pieces, depth):
     normed_ref, doc_ref, doc_column_ref = refs[:3]
-    norm_out, context_out, weights, projected, raised, sem = refs[-6:]
-    copies = place_pieces(refs[3:-6], weights, sem)
+    weights, projected, raised, sem, share_sem = refs[-5:]
+    copies = place_pieces(refs[3 : 3 + pieces], weights, sem)
+    outputs = refs[3 + pieces : -5]
+    moves = []
+    if depth:
+        moves = place_shares(*outputs[:2], *outputs[-2:], share_sem, depth)
+        outputs = outputs[2:]
+    norm_out, context_out = outputs[:2]
     for copy in copies:
+        copy.start()
+    for copy in moves:
         copy.start()
     width = normed_ref.shape[1]
     blocks, length = doc_ref.shape
@@ -174,30 +206,41 @@
             mixed = dot((members[b] * shares[i]).astype(bf16), values, ((1,), (0,)))
             both = jnp.where(lane[: 2 * SEGS] < HEAD, mixed[: 2 * SEGS], mixed[2 * SEGS :])
             context_out[b * SEGS : (b + 1) * SEGS, n : n + pair] = both[:SEGS] / lengths[b]
-
-
-def attention(normed, doc_ids, pieces):
+    for copy in moves:
+        copy.wait()
+
+
+def attention(normed, doc_ids, pieces, shares, depth, hidden):
     tokens, width = normed.shape
     blocks, length = doc_ids.shape
     vmem, anywhere = pl.BlockSpec(memory_space=pltpu.VMEM), pl.BlockSpec(memory_space=pl.ANY)
     pooled = jax.ShapeDtypeStruct((blocks * SEGS, width), f32)
+    placed, moves = (), 1
+    if shares:
+        count, _, lanes = shares[0].shape
+        placed = (
+            jax.ShapeDtypeStruct((2, width, lanes), bf16),
+            jax.ShapeDtypeStruct((2, hidden, width), bf16),
+        )
+        moves = CORES * count * (1 + width // lanes)
     flops = 2 * tokens * width * 3 * width + 6 * tokens * length * width
     return pl.pallas_call(
-        attention_kernel,
-        out_shape=(pooled, pooled),
-        in_specs=[vmem] * 3 + [anywhere] * len(pieces),
-        out_specs=(vmem, vmem),
+        functools.partial(attention_kernel, pieces=len(pieces), depth=depth if shares else 0),
+        out_shape=(pooled, pooled) + placed,
+        in_specs=[vmem] * 3 + [anywhere] * (len(pieces) + len(shares)),
+        out_specs=(vmem,) * (2 + len(placed)),
         scratch_shapes=[
             pltpu.VMEM((3 * width, width), bf16),
             pltpu.VMEM((tokens, 3 * width), bf16),
             pltpu.VMEM((width // (2 * HEAD), 2 * length, length), bf16),
             pltpu.SemaphoreType.DMA((len(pieces),)),
+            pltpu.SemaphoreType.DMA((moves,)),
         ],
         cost_estimate=pl.CostEstimate(
             flops=flops, bytes_accessed=8 * width * width, transcendentals=tokens * length * width // HEAD
         ),
         name="attention",
-    )(normed, doc_ids, doc_ids.T, *pieces)
+    )(normed, doc_ids, doc_ids.T, *pieces, *shares)
 
 
 def structure_kernel(mine, swapped, links, table, *, fan, slot_count, made):
@@ -207,7 +250,11 @@
     lanes = texts * rows
     capacity = rows // texts
     text, graph = lax.axis_index("text"), lax.axis_index("graph")
-    facts = [(swapped if d % CORES else mine)[d // CORES].astype(f32) for d in range(graphs)]
+    skip = texts * made
+    facts = [
+        (swapped if d % CORES else mine)[d // CORES, skip:, :lanes].astype(f32)
+        for d in range(graphs)
+    ]
     tails = jnp.concatenate([each[fan : fan + 1] for each in facts]).astype(jnp.int32)
     lane = lax.broadcasted_iota(jnp.int32, (graphs, lanes), 1)
 
@@ -255,8 +302,9 @@
             links[t, d * rows : (d + 1) * rows, :] = linked.astype(bf16)
 
 
-def node_kernel(mine, swapped, up_mine, up_swapped, table, links, one, two, out, own, live_out, *refs, fan):
-    first_self, first_next, up_self, up_next, live, kept = refs
+def node_kernel(mine, swapped, up_mine, up_swapped, table, links, one, two, *refs, fan):
+    first_self, first_next, up_self, up_next, live, kept = refs[-6:]
+    own, live_out = refs[-8:-6]
     texts, nodes, _ = links.shape
     graphs = table.shape[0]
     rows = nodes // graphs
@@ -266,7 +314,7 @@
     for d in range(graphs):
         chosen = table[d]
         values = (swapped if d % CORES else mine)[d // CORES]
-        ups = (up_swapped if d % CORES else up_mine)[d // CORES]
+        ups = (up_swapped if d % CORES else up_mine)[d // CORES, : texts * made]
         for target, value in (
             (live, ones),
             (first_self, values[:, :hidden]),
@@ -294,10 +342,12 @@
         kept[3, at, :] = (dot(linked[:, :rows], grad, ((0,), (0,))) / fan).astype(bf16)
     state = dot(kept[0], two[0], ((1,), (0,))) + dot(kept[1], two[1], ((1,), (0,)))
     back = [dot(table[0], kept[i], ((0,), (0,))).astype(bf16) for i in (2, 3)]
-    returned = dot(back[0], one[0], ((1,), (1,))) + dot(back[1], one[1], ((1,), (1,)))
-    for t in range(texts):
-        out[t, :rows, :] = state[t * rows : (t + 1) * rows].astype(bf16)
-        out[t, rows:, :] = returned[t * made : (t + 1) * made].astype(bf16)
+    returned = dot(back[0], one[0, :, :hidden], ((1,), (1,))) + dot(
+        back[1], one[1, :, :hidden], ((1,), (1,))
+    )
+    for t in range(1, texts):
+        refs[t - 1][:rows, :] = state[t * rows : (t + 1) * rows].astype(bf16)
+        refs[t - 1][rows:, :] = returned[t * made : (t + 1) * made].astype(bf16)
     own[:rows, :] = state[:rows]
     own[rows:, :] = returned[:made]
     live_out[...] = live[0, :rows, :].astype(f32)
@@ -306,7 +356,7 @@
 def unpack_kernel(mine, swapped, one, two, *, depth, share):
     graph = lax.axis_index("graph")
     graphs = CORES * mine.shape[0]
-    hidden, width = two.shape[1:]
+    width = two.shape[2]
     lanes = mine.shape[2]
     same = graph % CORES == 0
     for g in range(graphs):
@@ -314,7 +364,7 @@
         near, far = mine[z], swapped[z]
         got = jnp.where(same == (g % CORES == 0), near, far)
         half, j = g // (graphs // 2), g % (graphs // 2)
-        one[half, j * depth : (j + 1) * depth, :] = got[:depth, :hidden]
+        one[half, j * depth : (j + 1) * depth, :] = got[:depth]
         for m in range(width // lanes):
             part = got[depth + m * share : depth + (m + 1) * share]
             two[half, j * share : (j + 1) * share, m * lanes : (m + 1) * lanes] = part
@@ -325,7 +375,7 @@
     return pl.pallas_call(
         functools.partial(unpack_kernel, depth=depth, share=share),
         out_shape=(
-            jax.ShapeDtypeStruct((2, width, hidden), bf16),
+            jax.ShapeDtypeStruct((2, width, mine.shape[2]), bf16),
             jax.ShapeDtypeStruct((2, hidden, width), bf16),
         ),
         in_specs=[vmem] * 2,
@@ -360,18 +410,43 @@
     hidden, width = two.shape[1:]
     return pl.pallas_call(
         functools.partial(node_kernel, fan=fan),
-        out_shape=(
-            jax.ShapeDtypeStruct((texts, rows + made, width), bf16),
+        out_shape=[jax.ShapeDtypeStruct((rows + made, width), bf16)] * (texts - 1)
+        + [
             jax.ShapeDtypeStruct((rows + made, width), f32),
             jax.ShapeDtypeStruct((rows, 128), f32),
-        ),
+        ],
         in_specs=[vmem] * len(arrays),
-        out_specs=(vmem,) * 3,
+        out_specs=[vmem] * (texts + 1),
         scratch_shapes=[pltpu.VMEM((texts, nodes, hidden), bf16)] * 4
         + [pltpu.VMEM((texts, nodes, 128), bf16), pltpu.VMEM((4, texts * rows, hidden), bf16)],
         cost_estimate=pl.CostEstimate(flops=10**9, bytes_accessed=10**6, transcendentals=10**6),
         name="nodes",
     )(*arrays)
+
+
+def combine_kernel(own, live, *refs):
+    states, grads = refs[-2:]
+    rows = states.shape[0]
+    total = own[...]
+    for part in refs[:-2]:
+        total += part[...].astype(f32)
+    states[...] = (live[:, :1] * total[:rows]).astype(bf16)
+    grads[...] = total[rows:].astype(bf16)
+
+
+def combine(own, live, got):
+    vmem = pl.BlockSpec(memory_space=pltpu.VMEM)
+    rows, width = live.shape[0], own.shape[1]
+    return pl.pallas_call(
+        combine_kernel,
+        out_shape=(
+            jax.ShapeDtypeStruct((rows, width), bf16),
+            jax.ShapeDtypeStruct((own.shape[0] - rows, width), bf16),
+        ),
+        in_specs=[vmem] * (2 + len(got)),
+        out_specs=(vmem, vmem),
+        name="combine",
+    )(own, live, *got)
 
 
 def local(
@@ -398,6 +473,8 @@
     fan = neighbours.shape[1]
     slot_count = boundary.shape[1]
     i32 = jnp.int32
+    tail_count = boundary.size + made
+    dense = texts * rows == 128 and tail_count == rows and capacity * texts == rows
 
     qkv_shard, out_shard = attn_qkv.T, attn_out.T
     qkv_fetched = fetch_text(qkv_shard, core)
@@ -420,13 +497,24 @@
     sage_fetched = fetch_graph(packed)
 
     tail = jnp.concatenate([boundary.reshape(-1), owner_text.reshape(-1)])
-    tail_count = tail.shape[0]
     tail = jnp.pad(tail, (0, -tail_count % rows)).reshape(-1, rows)
     facts = jnp.concatenate([neighbours.T, tail], axis=0).astype(bf16)
     fact_rows = facts.shape[0]
     facts = jnp.pad(facts, ((0, rows - fact_rows), (0, -rows % 128)))
     outset = jnp.concatenate([out_grad, facts], axis=1)
     outset = [outset] + [over_text(outset, k) for k in range(1, texts)]
+    shares = swap_cores(sage_fetched)
+    normed = layer_norm(tokens, in_gain, in_bias)
+    if dense:
+        pooled_norm, pooled_context, one, two = attention(
+            normed, doc_ids, qkv_pieces, shares, depth, hidden
+        )
+    else:
+        pooled_norm, pooled_context = attention(normed, doc_ids, qkv_pieces, (), depth, hidden)
+        one, two = unpack(*shares, depth, share, hidden, width)
+    out_fetched, outset, pooled_context = lax.optimization_barrier(
+        (out_fetched, outset, pooled_context)
+    )
     grads = jnp.concatenate([part[:, :width] for part in outset], axis=0)
     facts = jnp.concatenate([part[:fact_rows, width : width + rows] for part in outset], axis=1)
 
@@ -446,14 +534,8 @@
     own_places = slot_places(tail_of(facts)[:, tail_count - made : tail_count])
     own_table = (own_places == jnp.arange(texts * rows, dtype=i32)[:, None]).astype(bf16)
     wide = 2 * hidden
-    facts_fetched = fetch_graph(facts)
-
-    one, two = unpack(*swap_cores(sage_fetched), depth, share, hidden, width)
-    normed = layer_norm(tokens, in_gain, in_bias)
-    pooled_norm, pooled_context = attention(normed, doc_ids, qkv_pieces)
-    out_fetched, facts_fetched, pooled_context = lax.optimization_barrier(
-        (out_fetched, facts_fetched, pooled_context)
-    )
+    facts_fetched = () if dense else fetch_graph(facts)
+
     out_pieces = pieces_of(out_shard, out_fetched)
     out_proj = assemble(out_pieces, text, core)
     embedded = dot(pooled_context.astype(bf16), out_proj, ((1,), (1,)))
@@ -463,28 +545,24 @@
     up = jnp.concatenate(
         [dot(live_grad, two[0], ((1,), (1,))), dot(live_grad, two[1], ((1,), (1,)))], axis=1
     ).astype(bf16)
+    if dense:
+        up = jnp.concatenate([up, jnp.pad(facts, ((0, 0), (0, wide - facts.shape[1])))])
     up_fetched = fetch_graph(up)
     gathered = jnp.concatenate(
         [embedded] + [over_text(embedded, k) for k in range(1, texts)], axis=0
     )
     first = jnp.concatenate(
-        [dot(gathered, one[0], ((1,), (0,))), dot(gathered, one[1], ((1,), (0,)))], axis=1
+        [dot(gathered, one[i], ((1,), (0,)))[:, :hidden] for i in range(2)], axis=1
     ).astype(bf16)
     first_fetched = fetch_graph(first)
 
-    if texts * rows == 128 and tail_count == rows and capacity * texts == rows:
+    if dense:
+        ups = swap_cores(up_fetched)
         links, table = structure(
-            *swap_cores(facts_fetched),
-            texts,
-            graphs,
-            rows,
-            fan=fan,
-            slot_count=slot_count,
-            made=made,
+            *ups, texts, graphs, rows, fan=fan, slot_count=slot_count, made=made
         )
-        parts = (*swap_cores(first_fetched), *swap_cores(up_fetched))
-        outgoing, total, live = node_stage_parts((*parts, table, links, one, two), fan)
-        live = live[:, :1]
+        parts = (*swap_cores(first_fetched), *ups)
+        *outgoing, total, live = node_stage_parts((*parts, table, links, one, two), fan)
     else:
         facts = share_cores(facts_fetched)
         ups = share_cores(up_fetched)
@@ -548,18 +626,17 @@
             forth[:, hidden:], two[1], ((1,), (0,))
         )
         back = dot(own_table, back.reshape(texts * rows, wide), ((0,), (0,))).astype(bf16)
-        grad_part = dot(back[:, :hidden], one[0], ((1,), (1,))) + dot(
-            back[:, hidden:], one[1], ((1,), (1,))
+        grad_part = dot(back[:, :hidden], one[0, :, :hidden], ((1,), (1,))) + dot(
+            back[:, hidden:], one[1, :, :hidden], ((1,), (1,))
         )
 
         final = jnp.concatenate(
             [state_part.reshape(texts, rows, width), grad_part.reshape(texts, made, width)], axis=1
         )
-        total, outgoing, live = final[0], final.astype(bf16), live[0]
-    for k in range(1, texts):
-        total = total + over_text(outgoing[k], k).astype(f32)
-    node_states = (live * total[:rows]).astype(bf16)
-    return (node_states, total[rows:].astype(bf16))
+        total, outgoing = final[0], list(final[1:].astype(bf16))
+        live = jnp.broadcast_to(live[0], (rows, 128))
+    got = [over_text(outgoing[k - 1], k) for k in range(1, texts)]
+    return combine(total, live, got)
 
 
 def solution(mesh):

time: 117 us -> 103 us (0.88)
  waiting for transfers between devices: 42.7 us -> 32.6 us
  starting transfers between devices: 36.1 us -> 32.8 us
  other arithmetic: 7.85 us -> 5.63 us
    ppermute x20 -> x16, waiting for transfers between devices: 19.9 us -> 6.59 us  [over_graph(): return lax.ppermute(array, 'graph', [(i, i ^ step) for i in range(count)])]
    ppermute x2, waiting for transfers between devices: 14.9 us -> 17.2 us  [over_pair(): return lax.ppermute(array, ('text', 'graph'), moves)]
    ppermute x20 -> x16, starting transfers between devices: 17.9 us -> 15.8 us  [over_graph(): return lax.ppermute(array, 'graph', [(i, i ^ step) for i in range(count)])]
    slice x2 -> x0, local copies, waits for them, and re-layouts: 1.44 us -> none  [the longest x1 0.83 us: local(): live = live[:, :1]]
    unnamed x44, local copies, waits for them, and re-layouts: 3.63 us -> 5 us
  transfers between devices with their start and end apart: 33 -> 29, of which waited for: 14 -> 9; matrix products, arithmetic and copies ran while one was open for 6% -> 9% of each run, Pallas kernels for 11% -> 12%
where the time goes in v2:
time: 103 us; the launch traced here: 102 us
  starting transfers between devices  32.8 us (32%)
  waiting for transfers between devices  32.6 us (32%)
  Pallas kernels  19.2 us (19%)
  local copies, waits for them, and re-layouts  9 us (9%)
  other arithmetic  5.63 us (5%)
  matrix products  1.74 us (2%)
  between operations  1.14 us (1%)
    ppermute x2, waiting for transfers between devices, over_pair(): return lax.ppermute(array, ('text', 'graph'), moves)  17.2 us
    ppermute x11, starting transfers between devices, over_text(): return lax.ppermute(array, 'text', [(i, i ^ step) for i in range(count)])  15.9 us
    ppermute x16, starting transfers between devices, over_graph(): return lax.ppermute(array, 'graph', [(i, i ^ step) for i in range(count)])  15.8 us
    pallas_call x1, Pallas kernels, attention(): pl.pallas_call(functools.partial(attention_kernel, pieces=len(pieces), de...  9.37 us
    ppermute x11, waiting for transfers between devices, over_text(): return lax.ppermute(array, 'text', [(i, i ^ step) for i in range(count)])  8.8 us
    ppermute x16, waiting for transfers between devices, over_graph(): return lax.ppermute(array, 'graph', [(i, i ^ step) for i in range(count)])  6.59 us
    pallas_call x1, Pallas kernels, node_stage_parts(): pl.pallas_call(functools.partial(node_kernel, fan=fan), out_shape=[jax.Sh...  5.36 us
    unnamed x44, local copies, waits for them, and re-layouts  5 us
  transfers between devices with their start and end apart: 29, of which 9 were waited for; matrix products, arithmetic and copies ran while one was open for 9% of the time, Pallas kernels for 12%

profile of v2, /device:TPU:0, one launch (start us, length us, event | category | flops | bytes accessed | tf_op | source)
XLA Modules:
  0.0 102.1 jit_solution(2110127465972202432)
XLA Ops:
  2.7 3.1 %collective-permute-start.9 = (bf16[336,256]{1,0:T(8,128)(2,1)S(1)}, bf16[336,256]{1,0:T(8,128)(2,1)S(1)}, u32[]{:S(2)}, u32[]{:S(2)}) collective-permute-start(bf16[336,256]{1,0:T(8,128)(2,1)S(1)} %get-tuple-element.56), channel_id=1, source_target_pairs={{0,2},{1,3},{2,0},{3,1},{4,6},{5,7},{6,4},{7,5},{8,10},{9,11},{10,... | collective-permute-start | bytes 516104 | tf_op jit(solution)/shard_map/ppermute | solution.py:31
  5.8 2.6 %collective-permute-start.10 = (bf16[336,256]{1,0:T(8,128)(2,1)S(1)}, bf16[336,256]{1,0:T(8,128)(2,1)S(1)}, u32[]{:S(2)}, u32[]{:S(2)}) collective-permute-start(bf16[336,256]{1,0:T(8,128)(2,1)S(1)} %get-tuple-element.56), channel_id=1, source_target_pairs={{0,4},{1,5},{2,6},{3,7},{4,0},{5,1},{6,2},{7,3},{8,12},{9,13},{10,... | collective-permute-start | bytes 516104 | tf_op jit(solution)/shard_map/ppermute | solution.py:31
  8.5 2.7 %collective-permute-start.7 = (bf16[576,384]{1,0:T(8,128)(2,1)S(1)}, bf16[576,384]{1,0:T(8,128)(2,1)}, u32[]{:S(2)}, u32[]{:S(2)}) collective-permute-start(bf16[576,384]{1,0:T(8,128)(2,1)S(1)} %dynamic-slice_bitcast_fusion), channel_id=1, source_target_pairs={{0,24},{8,16},{16,8},{24,0},{1,25},{9,17},{17,9},{25,1},{2,26},{10... | collective-permute-start | bytes 1327112 | tf_op jit(solution)/shard_map/ppermute | solution.py:26
  13.3 17.2 %collective-permute-done.5.refs_4_ = bf16[576,768]{1,0:T(8,128)(2,1)} collective-permute-done((bf16[576,768]{1,0:T(8,128)(2,1)S(1)}, bf16[576,768]{1,0:T(8,128)(2,1)}, u32[]{:S(2)}, u32[]{:S(2)}) %collective-permute-start.5) | collective-permute-done | bytes 884768 | tf_op jit(solution)/shard_map/ppermute | solution.py:40
  30.5 1.4 %copy.19 = s32[4,128]{0,1:T(8,128)} copy(s32[4,128]{1,0:T(4,128)} %refs_1_.1) | data formatting | bytes 4096 | tf_op args[1]
  32.0 1.5 %collective-permute-start.2 = (bf16[32,896]{1,0:T(8,128)(2,1)S(1)}, bf16[32,896]{1,0:T(8,128)(2,1)}, u32[]{:S(2)}, u32[]{:S(2)}) collective-permute-start(bf16[32,896]{1,0:T(8,128)(2,1)S(1)} %pad_maximum_fusion.7), channel_id=1, source_target_pairs={{0,8},{8,0},{16,24},{24,16},{1,9},{9,1},{17,25},{25,17},{2,10},{10... | collective-permute-start | bytes 172040 | tf_op jit(solution)/shard_map/ppermute | solution.py:26
  35.6 1.9 %fusion.5.refs_0_ = bf16[512,768]{1,0:T(8,128)(2,1)} fusion(bf16[512,768]{1,0:T(8,128)(2,1)S(1)} %copy-done.1, f32[768]{0:T(1024)} %param.15, f32[768]{0:T(1024)} %param.14, f32[512]{0:T(512)S(1)} %add_rsqrt_fusion, f32[512]{0:T(512)S(1)} %broadcast_multiply_fusion), kind=kLoop, calls=%fused_computation.7 | loop fusion | flops 2359296 | bytes 1583104 | tf_op jit(solution)/shard_map/convert_element_type | solution.py:117
  37.6 1.3 %collective-permute-start.3 = (bf16[32,896]{1,0:T(8,128)(2,1)S(1)}, bf16[32,896]{1,0:T(8,128)(2,1)S(1)}, u32[]{:S(2)}, u32[]{:S(2)}) collective-permute-start(bf16[32,896]{1,0:T(8,128)(2,1)S(1)} %pad_maximum_fusion.7), channel_id=1, source_target_pairs={{0,16},{8,24},{16,0},{24,8},{1,17},{9,25},{17,1},{25,9},{2,18},{10... | collective-permute-start | bytes 172040 | tf_op jit(solution)/shard_map/ppermute | solution.py:26
  38.9 1.7 %collective-permute-start.4 = (bf16[32,896]{1,0:T(8,128)(2,1)S(1)}, bf16[32,896]{1,0:T(8,128)(2,1)S(1)}, u32[]{:S(2)}, u32[]{:S(2)}) collective-permute-start(bf16[32,896]{1,0:T(8,128)(2,1)S(1)} %pad_maximum_fusion.7), channel_id=1, source_target_pairs={{0,24},{8,16},{16,8},{24,0},{1,25},{9,17},{17,9},{25,1},{2,26},{10... | collective-permute-start | bytes 172040 | tf_op jit(solution)/shard_map/ppermute | solution.py:26
  41.8 9.4 %attention.1 = (f32[16,768]{1,0:T(8,128)}, f32[16,768]{1,0:T(8,128)}, bf16[2,768,256]{2,1,0:T(8,128)(2,1)}, bf16[2,192,768]{2,1,0:T(8,128)(2,1)}) custom-call(bf16[512,768]{1,0:T(8,128)(2,1)} %fusion.5.refs_0_, s32[4,128]{1,0:T(4,128)} %refs_1_.1, s32[128,4]{1,0:T(8,128)} %bitcast.65, bf16[576,768]{1,0:T(8,128)(2,1)} %bitcast.59, ...), custom_call_target="tpu_custom_call" | custom-call | flops 2113929216 | bytes 4718592 | tf_op jit(solution)/shard_map/attention/pallas_call | solution.py:227
  59.4 3.5 %collective-permute-start.23 = (bf16[80,384]{1,0:T(8,128)(2,1)S(1)}, bf16[80,384]{1,0:T(8,128)(2,1)S(1)}, u32[]{:S(2)}, u32[]{:S(2)}) collective-permute-start(bf16[80,384]{1,0:T(8,128)(2,1)S(1)} %fusion.15), channel_id=1, source_target_pairs={{0,4},{1,5},{2,6},{3,7},{4,0},{5,1},{6,2},{7,3},{8,12},{9,13},{10,... | collective-permute-start | bytes 184328 | tf_op jit(solution)/shard_map/ppermute | solution.py:31
  64.1 1.4 %collective-permute-start.16 = (bf16[16,768]{1,0:T(8,128)(2,1)S(1)}, bf16[16,768]{1,0:T(8,128)(2,1)S(1)}, u32[]{:S(2)}, u32[]{:S(2)}) collective-permute-start(bf16[16,768]{1,0:T(8,128)(2,1)S(1)} %add_convert_fusion), channel_id=1, source_target_pairs={{0,16},{8,24},{16,0},{24,8},{1,17},{9,25},{17,1},{25,9},{2,18},{10... | collective-permute-start | bytes 73736 | tf_op jit(solution)/shard_map/ppermute | solution.py:26
  65.5 1.5 %collective-permute-done.15 = bf16[16,768]{1,0:T(8,128)(2,1)S(1)} collective-permute-done((bf16[16,768]{1,0:T(8,128)(2,1)S(1)}, bf16[16,768]{1,0:T(8,128)(2,1)S(1)}, u32[]{:S(2)}, u32[]{:S(2)}) %collective-permute-start.15) | collective-permute-done | bytes 24608 | tf_op jit(solution)/shard_map/ppermute | solution.py:26
  67.0 1.7 %collective-permute-start.17 = (bf16[16,768]{1,0:T(8,128)(2,1)S(1)}, bf16[16,768]{1,0:T(8,128)(2,1)S(1)}, u32[]{:S(2)}, u32[]{:S(2)}) collective-permute-start(bf16[16,768]{1,0:T(8,128)(2,1)S(1)} %add_convert_fusion), channel_id=1, source_target_pairs={{0,24},{8,16},{16,8},{24,0},{1,25},{9,17},{17,9},{25,1},{2,26},{10... | collective-permute-start | bytes 73736 | tf_op jit(solution)/shard_map/ppermute | solution.py:26
  68.8 3.0 %collective-permute-done.17 = bf16[16,768]{1,0:T(8,128)(2,1)S(1)} collective-permute-done((bf16[16,768]{1,0:T(8,128)(2,1)S(1)}, bf16[16,768]{1,0:T(8,128)(2,1)S(1)}, u32[]{:S(2)}, u32[]{:S(2)}) %collective-permute-start.17) | collective-permute-done | bytes 24608 | tf_op jit(solution)/shard_map/ppermute | solution.py:26
  72.6 3.8 %collective-permute-start.19 = (bf16[64,384]{1,0:T(8,128)(2,1)S(1)}, bf16[64,384]{1,0:T(8,128)(2,1)S(1)}, u32[]{:S(2)}, u32[]{:S(2)}) collective-permute-start(bf16[64,384]{1,0:T(8,128)(2,1)S(1)} %pad_maximum_fusion.8), channel_id=1, source_target_pairs={{0,4},{1,5},{2,6},{3,7},{4,0},{5,1},{6,2},{7,3},{8,12},{9,13},{10,... | collective-permute-start | bytes 147464 | tf_op jit(solution)/shard_map/ppermute | solution.py:31
  76.8 2.6 %collective-permute-done.19 = bf16[64,384]{1,0:T(8,128)(2,1)S(1)} collective-permute-done((bf16[64,384]{1,0:T(8,128)(2,1)S(1)}, bf16[64,384]{1,0:T(8,128)(2,1)S(1)}, u32[]{:S(2)}, u32[]{:S(2)}) %collective-permute-start.19) | collective-permute-done | bytes 49184 | tf_op jit(solution)/shard_map/ppermute | solution.py:31
  79.4 2.9 %collective-permute-done.20 = bf16[64,384]{1,0:T(8,128)(2,1)S(1)} collective-permute-done((bf16[64,384]{1,0:T(8,128)(2,1)S(1)}, bf16[64,384]{1,0:T(8,128)(2,1)S(1)}, u32[]{:S(2)}, u32[]{:S(2)}) %collective-permute-start.20) | collective-permute-done | bytes 49184 | tf_op jit(solution)/shard_map/ppermute | solution.py:31
  83.2 2.7 %structure.1 = (bf16[4,256,256]{2,1,0:T(8,128)(2,1)}, bf16[8,128,64]{2,1,0:T(8,128)(2,1)}) custom-call(bf16[4,80,384]{2,1,0:T(8,128)(2,1)} %copy-done.4, bf16[4,80,384]{2,1,0:T(8,128)(2,1)} %copy-done.16), custom_call_target="tpu_custom_call" | custom-call | flops 1000000000 | bytes 1000000 | tf_op jit(solution)/shard_map/structure/pallas_call | solution.py:391
  86.6 5.4 %nodes.1 = (bf16[48,768]{1,0:T(8,128)(2,1)}, bf16[48,768]{1,0:T(8,128)(2,1)}, bf16[48,768]{1,0:T(8,128)(2,1)}, f32[48,768]{1,0:T(8,128)}, f32[32,128]{1,0:T(8,128)}) custom-call(bf16[4,64,384]{2,1,0:T(8,128)(2,1)} %copy-done.6, bf16[4,64,384]{2,1,0:T(8,128)(2,1)} %copy-done.17, bf16[4,80,384]{2,1,0:T(8,128)(2,1)} %copy-done.4, ...), custom_call_target="tpu_custom_call" | custom-call | flops 1000000000 | bytes 1000000 | tf_op jit(solution)/shard_map/nodes/pallas_call | solution.py:411
  92.8 1.4 %collective-permute-start.27 = (bf16[48,768]{1,0:T(8,128)(2,1)}, bf16[48,768]{1,0:T(8,128)(2,1)S(1)}, u32[]{:S(2)}, u32[]{:S(2)}) collective-permute-start(bf16[48,768]{1,0:T(8,128)(2,1)} %get-tuple-element.40), channel_id=1, source_target_pairs={{0,16},{8,24},{16,0},{24,8},{1,17},{9,25},{17,1},{25,9},{2,18},{10... | collective-permute-start | bytes 221192 | tf_op jit(solution)/shard_map/ppermute | solution.py:26
  95.4 1.4 %collective-permute-done.26.refs_0_ = bf16[48,768]{1,0:T(8,128)(2,1)S(1)} collective-permute-done((bf16[48,768]{1,0:T(8,128)(2,1)}, bf16[48,768]{1,0:T(8,128)(2,1)S(1)}, u32[]{:S(2)}, u32[]{:S(2)}) %collective-permute-start.26) | collective-permute-done | bytes 73760 | tf_op jit(solution)/shard_map/ppermute | solution.py:26
  97.4 2.3 %collective-permute-done.28.refs_2_ = bf16[48,768]{1,0:T(8,128)(2,1)S(1)} collective-permute-done((bf16[48,768]{1,0:T(8,128)(2,1)}, bf16[48,768]{1,0:T(8,128)(2,1)S(1)}, u32[]{:S(2)}, u32[]{:S(2)}) %collective-permute-start.28) | collective-permute-done | bytes 73760 | tf_op jit(solution)/shard_map/ppermute | solution.py:26
  100.3 1.7 %combine.1 = (bf16[32,768]{1,0:T(8,128)(2,1)}, bf16[16,768]{1,0:T(8,128)(2,1)}) custom-call(f32[48,768]{1,0:T(8,128)} %get-tuple-element.37.own, f32[32,128]{1,0:T(8,128)} %get-tuple-element.38.live, bf16[48,768]{1,0:T(8,128)(2,1)} %copy-done.7, bf16[48,768]{1,0:T(8,128)(2,1)} %copy-done.8, bf16[48,768]{1,0:T(8,128)(2,1)} %copy-done.9), custom_call_target="tpu_custom_call" | custom-call | tf_op jit(solution)/shard_map/combine/pallas_call | solution.py:440
  (140 shorter events, 22.7 us)
Async XLA Ops:
  2.7 29.2 %collective-permute-start.9 = (bf16[336,256]{1,0:T(8,128)(2,1)S(1)}, bf16[336,256]{1,0:T(8,128)(2,1)S(1)}, u32[]{:S(2)}, u32[]{:S(2)}) collective-permute-start(bf16[336,256]{1,0:T(8,128)(2,1)S(1)} %get-tuple-element.56), channel_id=1, source_target_pairs={{0,2},{1,3},{2,0},{3,1},{4,6},{5,7},{6,4},{7,5},{8,10},{9,11},{10,... | collective-permute-start | bytes 516104 | tf_op jit(solution)/shard_map/ppermute | solution.py:31
  5.8 27.6 %collective-permute-start.10 = (bf16[336,256]{1,0:T(8,128)(2,1)S(1)}, bf16[336,256]{1,0:T(8,128)(2,1)S(1)}, u32[]{:S(2)}, u32[]{:S(2)}) collective-permute-start(bf16[336,256]{1,0:T(8,128)(2,1)S(1)} %get-tuple-element.56), channel_id=1, source_target_pairs={{0,4},{1,5},{2,6},{3,7},{4,0},{5,1},{6,2},{7,3},{8,12},{9,13},{10,... | collective-permute-start | bytes 516104 | tf_op jit(solution)/shard_map/ppermute | solution.py:31
  8.4 25.6 %collective-permute-start.11 = (bf16[336,256]{1,0:T(8,128)(2,1)S(1)}, bf16[336,256]{1,0:T(8,128)(2,1)}, u32[]{:S(2)}, u32[]{:S(2)}) collective-permute-start(bf16[336,256]{1,0:T(8,128)(2,1)S(1)} %get-tuple-element.56), channel_id=1, source_target_pairs={{0,6},{1,7},{2,4},{3,5},{4,2},{5,3},{6,0},{7,1},{8,14},{9,15},{10,... | collective-permute-start | bytes 516104 | tf_op jit(solution)/shard_map/ppermute | solution.py:31
  8.5 26.6 %collective-permute-start.7 = (bf16[576,384]{1,0:T(8,128)(2,1)S(1)}, bf16[576,384]{1,0:T(8,128)(2,1)}, u32[]{:S(2)}, u32[]{:S(2)}) collective-permute-start(bf16[576,384]{1,0:T(8,128)(2,1)S(1)} %dynamic-slice_bitcast_fusion), channel_id=1, source_target_pairs={{0,24},{8,16},{16,8},{24,0},{1,25},{9,17},{17,9},{25,1},{2,26},{10... | collective-permute-start | bytes 1327112 | tf_op jit(solution)/shard_map/ppermute | solution.py:26
  11.2 19.3 %collective-permute-start.5 = (bf16[576,768]{1,0:T(8,128)(2,1)S(1)}, bf16[576,768]{1,0:T(8,128)(2,1)}, u32[]{:S(2)}, u32[]{:S(2)}) collective-permute-start(bf16[576,768]{1,0:T(8,128)(2,1)S(1)} %bitcast.60), channel_id=1, source_target_pairs={{0,8},{1,17},{2,10},{3,19},{4,12},{5,21},{6,14},{7,23},{8,0},{9,25... | collective-permute-start | bytes 2654216 | tf_op jit(solution)/shard_map/ppermute | solution.py:40
  30.5 10.1 %collective-permute-start.6 = (bf16[576,768]{1,0:T(8,128)(2,1)}, bf16[576,768]{1,0:T(8,128)(2,1)}, u32[]{:S(2)}, u32[]{:S(2)}) collective-permute-start(bf16[576,768]{1,0:T(8,128)(2,1)} %collective-permute-done.5.refs_4_), channel_id=1, source_target_pairs={{0,1},{1,0},{2,3},{3,2},{4,5},{5,4},{6,7},{7,6},{8,9},{9,8},{10,11... | collective-permute-start | bytes 2654216 | tf_op jit(solution)/shard_map/ppermute | solution.py:31
  32.0 19.2 %collective-permute-start.2 = (bf16[32,896]{1,0:T(8,128)(2,1)S(1)}, bf16[32,896]{1,0:T(8,128)(2,1)}, u32[]{:S(2)}, u32[]{:S(2)}) collective-permute-start(bf16[32,896]{1,0:T(8,128)(2,1)S(1)} %pad_maximum_fusion.7), channel_id=1, source_target_pairs={{0,8},{8,0},{16,24},{24,16},{1,9},{9,1},{17,25},{25,17},{2,10},{10... | collective-permute-start | bytes 172040 | tf_op jit(solution)/shard_map/ppermute | solution.py:26
  33.5 17.8 %collective-permute-start = (bf16[192,768]{1,0:T(8,128)(2,1)S(1)}, bf16[192,768]{1,0:T(8,128)(2,1)S(1)}, u32[]{:S(2)}, u32[]{:S(2)}) collective-permute-start(bf16[192,768]{1,0:T(8,128)(2,1)S(1)} %bitcast.57), channel_id=1, source_target_pairs={{0,8},{1,17},{2,10},{3,19},{4,12},{5,21},{6,14},{7,23},{8,0},{9,25... | collective-permute-start | bytes 884744 | tf_op jit(solution)/shard_map/ppermute | solution.py:40
  37.6 13.6 %collective-permute-start.3 = (bf16[32,896]{1,0:T(8,128)(2,1)S(1)}, bf16[32,896]{1,0:T(8,128)(2,1)S(1)}, u32[]{:S(2)}, u32[]{:S(2)}) collective-permute-start(bf16[32,896]{1,0:T(8,128)(2,1)S(1)} %pad_maximum_fusion.7), channel_id=1, source_target_pairs={{0,16},{8,24},{16,0},{24,8},{1,17},{9,25},{17,1},{25,9},{2,18},{10... | collective-permute-start | bytes 172040 | tf_op jit(solution)/shard_map/ppermute | solution.py:26
  38.9 12.3 %collective-permute-start.4 = (bf16[32,896]{1,0:T(8,128)(2,1)S(1)}, bf16[32,896]{1,0:T(8,128)(2,1)S(1)}, u32[]{:S(2)}, u32[]{:S(2)}) collective-permute-start(bf16[32,896]{1,0:T(8,128)(2,1)S(1)} %pad_maximum_fusion.7), channel_id=1, source_target_pairs={{0,24},{8,16},{16,8},{24,0},{1,25},{9,17},{17,9},{25,1},{2,26},{10... | collective-permute-start | bytes 172040 | tf_op jit(solution)/shard_map/ppermute | solution.py:26
  40.6 10.6 %collective-permute-start.1 = (bf16[192,384]{1,0:T(8,128)(2,1)S(1)}, bf16[192,384]{1,0:T(8,128)(2,1)S(1)}, u32[]{:S(2)}, u32[]{:S(2)}) collective-permute-start(bf16[192,384]{1,0:T(8,128)(2,1)S(1)} %dynamic-slice_bitcast_fusion.1), channel_id=1, source_target_pairs={{0,24},{8,16},{16,8},{24,0},{1,25},{9,17},{17,9},{25,1},{2,26},{10... | collective-permute-start | bytes 442376 | tf_op jit(solution)/shard_map/ppermute | solution.py:26
  58.8 17.6 %collective-permute-start.22 = (bf16[80,384]{1,0:T(8,128)(2,1)S(1)}, bf16[80,384]{1,0:T(8,128)(2,1)S(1)}, u32[]{:S(2)}, u32[]{:S(2)}) collective-permute-start(bf16[80,384]{1,0:T(8,128)(2,1)S(1)} %fusion.15), channel_id=1, source_target_pairs={{0,2},{1,3},{2,0},{3,1},{4,6},{5,7},{6,4},{7,5},{8,10},{9,11},{10,... | collective-permute-start | bytes 184328 | tf_op jit(solution)/shard_map/ppermute | solution.py:31
  59.4 17.3 %collective-permute-start.23 = (bf16[80,384]{1,0:T(8,128)(2,1)S(1)}, bf16[80,384]{1,0:T(8,128)(2,1)S(1)}, u32[]{:S(2)}, u32[]{:S(2)}) collective-permute-start(bf16[80,384]{1,0:T(8,128)(2,1)S(1)} %fusion.15), channel_id=1, source_target_pairs={{0,4},{1,5},{2,6},{3,7},{4,0},{5,1},{6,2},{7,3},{8,12},{9,13},{10,... | collective-permute-start | bytes 184328 | tf_op jit(solution)/shard_map/ppermute | solution.py:31
  62.9 13.8 %collective-permute-start.24 = (bf16[80,384]{1,0:T(8,128)(2,1)S(1)}, bf16[80,384]{1,0:T(8,128)(2,1)S(1)}, u32[]{:S(2)}, u32[]{:S(2)}) collective-permute-start(bf16[80,384]{1,0:T(8,128)(2,1)S(1)} %fusion.15), channel_id=1, source_target_pairs={{0,6},{1,7},{2,4},{3,5},{4,2},{5,3},{6,0},{7,1},{8,14},{9,15},{10,... | collective-permute-start | bytes 184328 | tf_op jit(solution)/shard_map/ppermute | solution.py:31
  63.2 3.8 %collective-permute-start.15 = (bf16[16,768]{1,0:T(8,128)(2,1)S(1)}, bf16[16,768]{1,0:T(8,128)(2,1)S(1)}, u32[]{:S(2)}, u32[]{:S(2)}) collective-permute-start(bf16[16,768]{1,0:T(8,128)(2,1)S(1)} %add_convert_fusion), channel_id=1, source_target_pairs={{0,8},{8,0},{16,24},{24,16},{1,9},{9,1},{17,25},{25,17},{2,10},{10... | collective-permute-start | bytes 73736 | tf_op jit(solution)/shard_map/ppermute | solution.py:26
  64.1 4.7 %collective-permute-start.16 = (bf16[16,768]{1,0:T(8,128)(2,1)S(1)}, bf16[16,768]{1,0:T(8,128)(2,1)S(1)}, u32[]{:S(2)}, u32[]{:S(2)}) collective-permute-start(bf16[16,768]{1,0:T(8,128)(2,1)S(1)} %add_convert_fusion), channel_id=1, source_target_pairs={{0,16},{8,24},{16,0},{24,8},{1,17},{9,25},{17,1},{25,9},{2,18},{10... | collective-permute-start | bytes 73736 | tf_op jit(solution)/shard_map/ppermute | solution.py:26
  67.0 4.7 %collective-permute-start.17 = (bf16[16,768]{1,0:T(8,128)(2,1)S(1)}, bf16[16,768]{1,0:T(8,128)(2,1)S(1)}, u32[]{:S(2)}, u32[]{:S(2)}) collective-permute-start(bf16[16,768]{1,0:T(8,128)(2,1)S(1)} %add_convert_fusion), channel_id=1, source_target_pairs={{0,24},{8,16},{16,8},{24,0},{1,25},{9,17},{17,9},{25,1},{2,26},{10... | collective-permute-start | bytes 73736 | tf_op jit(solution)/shard_map/ppermute | solution.py:26
  72.2 4.6 %collective-permute-start.18 = (bf16[64,384]{1,0:T(8,128)(2,1)S(1)}, bf16[64,384]{1,0:T(8,128)(2,1)S(1)}, u32[]{:S(2)}, u32[]{:S(2)}) collective-permute-start(bf16[64,384]{1,0:T(8,128)(2,1)S(1)} %pad_maximum_fusion.8), channel_id=1, source_target_pairs={{0,2},{1,3},{2,0},{3,1},{4,6},{5,7},{6,4},{7,5},{8,10},{9,11},{10,... | collective-permute-start | bytes 147464 | tf_op jit(solution)/shard_map/ppermute | solution.py:31
  72.6 6.9 %collective-permute-start.19 = (bf16[64,384]{1,0:T(8,128)(2,1)S(1)}, bf16[64,384]{1,0:T(8,128)(2,1)S(1)}, u32[]{:S(2)}, u32[]{:S(2)}) collective-permute-start(bf16[64,384]{1,0:T(8,128)(2,1)S(1)} %pad_maximum_fusion.8), channel_id=1, source_target_pairs={{0,4},{1,5},{2,6},{3,7},{4,0},{5,1},{6,2},{7,3},{8,12},{9,13},{10,... | collective-permute-start | bytes 147464 | tf_op jit(solution)/shard_map/ppermute | solution.py:31
  76.4 5.9 %collective-permute-start.20 = (bf16[64,384]{1,0:T(8,128)(2,1)S(1)}, bf16[64,384]{1,0:T(8,128)(2,1)S(1)}, u32[]{:S(2)}, u32[]{:S(2)}) collective-permute-start(bf16[64,384]{1,0:T(8,128)(2,1)S(1)} %pad_maximum_fusion.8), channel_id=1, source_target_pairs={{0,6},{1,7},{2,4},{3,5},{4,2},{5,3},{6,0},{7,1},{8,14},{9,15},{10,... | collective-permute-start | bytes 147464 | tf_op jit(solution)/shard_map/ppermute | solution.py:31
  76.8 5.7 %collective-permute-start.25 = (bf16[4,80,384]{2,1,0:T(8,128)(2,1)S(1)}, bf16[4,80,384]{2,1,0:T(8,128)(2,1)S(1)}, u32[]{:S(2)}, u32[]{:S(2)}) collective-permute-start(bf16[4,80,384]{2,1,0:T(8,128)(2,1)S(1)} %pad_maximum_fusion.3.mine.up_mine), channel_id=1, source_target_pairs={{0,1},{1,0},{2,3},{3,2},{4,5},{5,4},{6,7},{7,6},{8,9},{9,8},{10,11... | collective-permute-start | bytes 737288 | tf_op jit(solution)/shard_map/ppermute | solution.py:31
  91.9 4.9 %collective-permute-start.26 = (bf16[48,768]{1,0:T(8,128)(2,1)}, bf16[48,768]{1,0:T(8,128)(2,1)S(1)}, u32[]{:S(2)}, u32[]{:S(2)}) collective-permute-start(bf16[48,768]{1,0:T(8,128)(2,1)} %get-tuple-element.39), channel_id=1, source_target_pairs={{0,8},{8,0},{16,24},{24,16},{1,9},{9,1},{17,25},{25,17},{2,10},{10... | collective-permute-start | bytes 221192 | tf_op jit(solution)/shard_map/ppermute | solution.py:26
  92.8 4.6 %collective-permute-start.27 = (bf16[48,768]{1,0:T(8,128)(2,1)}, bf16[48,768]{1,0:T(8,128)(2,1)S(1)}, u32[]{:S(2)}, u32[]{:S(2)}) collective-permute-start(bf16[48,768]{1,0:T(8,128)(2,1)} %get-tuple-element.40), channel_id=1, source_target_pairs={{0,16},{8,24},{16,0},{24,8},{1,17},{9,25},{17,1},{25,9},{2,18},{10... | collective-permute-start | bytes 221192 | tf_op jit(solution)/shard_map/ppermute | solution.py:26
  94.2 5.5 %collective-permute-start.28 = (bf16[48,768]{1,0:T(8,128)(2,1)}, bf16[48,768]{1,0:T(8,128)(2,1)S(1)}, u32[]{:S(2)}, u32[]{:S(2)}) collective-permute-start(bf16[48,768]{1,0:T(8,128)(2,1)} %get-tuple-element.41), channel_id=1, source_target_pairs={{0,24},{8,16},{16,8},{24,0},{1,25},{9,17},{17,9},{25,1},{2,26},{10... | collective-permute-start | bytes 221192 | tf_op jit(solution)/shard_map/ppermute | solution.py:26
  (25 other events, 112.6 us)

commit v3 on v2

--- a/solution.py
+++ b/solution.py
@@ -512,11 +512,10 @@
     else:
         pooled_norm, pooled_context = attention(normed, doc_ids, qkv_pieces, (), depth, hidden)
         one, two = unpack(*shares, depth, share, hidden, width)
-    out_fetched, outset, pooled_context = lax.optimization_barrier(
-        (out_fetched, outset, pooled_context)
-    )
+    out_fetched, pooled_context = lax.optimization_barrier((out_fetched, pooled_context))
     grads = jnp.concatenate([part[:, :width] for part in outset], axis=0)
-    facts = jnp.concatenate([part[:fact_rows, width : width + rows] for part in outset], axis=1)
+    facts = [part[:fact_rows, width : width + rows] for part in outset]
+    facts = jnp.concatenate(facts, axis=1)
 
     def tail_of(facts):
         tail = facts[..., fan:, :].reshape(facts.shape[:-2] + (fact_rows - fan, texts, rows))
@@ -551,9 +550,7 @@
     gathered = jnp.concatenate(
         [embedded] + [over_text(embedded, k) for k in range(1, texts)], axis=0
     )
-    first = jnp.concatenate(
-        [dot(gathered, one[i], ((1,), (0,)))[:, :hidden] for i in range(2)], axis=1
-    ).astype(bf16)
+    first = dot(gathered, one, ((1,), (1,)))[:, :, :hidden].reshape(-1, wide).astype(bf16)
     first_fetched = fetch_graph(first)
 
     if dense:

time: 103 us -> 92.4 us (0.90)
  waiting for transfers between devices: 32.6 us -> 24.3 us
  local copies, waits for them, and re-layouts: 9 us -> 7.6 us
  other arithmetic: 5.63 us -> 4.23 us
  starting transfers between devices: 32.8 us -> 33.9 us
    ppermute x2, waiting for transfers between devices: 17.2 us -> 4.28 us  [over_pair(): return lax.ppermute(array, ('text', 'graph'), moves)]
    ppermute x16, waiting for transfers between devices: 6.59 us -> 9.38 us  [over_graph(): return lax.ppermute(array, 'graph', [(i, i ^ step) for i in range(count)])]
    ppermute x2, starting transfers between devices: 1.07 us -> 3.14 us  [over_pair(): return lax.ppermute(array, ('text', 'graph'), moves)]
    ppermute x11, waiting for transfers between devices: 8.8 us -> 10.7 us  [over_text(): return lax.ppermute(array, 'text', [(i, i ^ step) for i in range(count)])]
    ppermute x11, starting transfers between devices: 15.9 us -> 14.7 us  [over_text(): return lax.ppermute(array, 'text', [(i, i ^ step) for i in range(count)])]
    squeeze x1 -> x0, local copies, waits for them, and re-layouts: 1.17 us -> none  [local(): one[i]]
    unnamed x44 -> x55, local copies, waits for them, and re-layouts: 5 us -> 5.98 us
  transfers between devices with their start and end apart: 29 -> 29, of which waited for: 9 -> 13; matrix products, arithmetic and copies ran while one was open for 9% -> 6% of each run, Pallas kernels for 12% -> 13%
where the time goes in v3:
time: 92.4 us; the launch traced here: 92.1 us
  starting transfers between devices  33.9 us (37%)
  waiting for transfers between devices  24.3 us (26%)
  Pallas kernels  19.2 us (21%)
  local copies, waits for them, and re-layouts  7.6 us (8%)
  other arithmetic  4.23 us (5%)
  matrix products  1.63 us (2%)
  between operations  1.16 us (1%)
    ppermute x16, starting transfers between devices, over_graph(): return lax.ppermute(array, 'graph', [(i, i ^ step) for i in range(count)])  16.1 us
    ppermute x11, starting transfers between devices, over_text(): return lax.ppermute(array, 'text', [(i, i ^ step) for i in range(count)])  14.7 us
    ppermute x11, waiting for transfers between devices, over_text(): return lax.ppermute(array, 'text', [(i, i ^ step) for i in range(count)])  10.7 us
    ppermute x16, waiting for transfers between devices, over_graph(): return lax.ppermute(array, 'graph', [(i, i ^ step) for i in range(count)])  9.38 us
    pallas_call x1, Pallas kernels, attention(): pl.pallas_call(functools.partial(attention_kernel, pieces=len(pieces), de...  9.37 us
    unnamed x55, local copies, waits for them, and re-layouts  5.98 us
    pallas_call x1, Pallas kernels, node_stage_parts(): pl.pallas_call(functools.partial(node_kernel, fan=fan), out_shape=[jax.Sh...  5.36 us
    ppermute x2, waiting for transfers between devices, over_pair(): return lax.ppermute(array, ('text', 'graph'), moves)  4.28 us
  transfers between devices with their start and end apart: 29, of which 13 were waited for; matrix products, arithmetic and copies ran while one was open for 6% of the time, Pallas kernels for 13%

profile of v3, /device:TPU:0, one launch (start us, length us, event | category | flops | bytes accessed | tf_op | source)
XLA Modules:
  0.0 92.1 jit_solution(9280169344324548844)
XLA Ops:
  2.7 5.1 %collective-permute-start.9 = (bf16[336,256]{1,0:T(8,128)(2,1)S(1)}, bf16[336,256]{1,0:T(8,128)(2,1)S(1)}, u32[]{:S(2)}, u32[]{:S(2)}) collective-permute-start(bf16[336,256]{1,0:T(8,128)(2,1)S(1)} %get-tuple-element.46), channel_id=1, source_target_pairs={{0,6},{1,7},{2,4},{3,5},{4,2},{5,3},{6,0},{7,1},{8,14},{9,15},{10,... | collective-permute-start | bytes 516104 | tf_op jit(solution)/shard_map/ppermute | solution.py:31
  8.5 1.6 %collective-permute-start.3 = (bf16[576,768]{1,0:T(8,128)(2,1)}, bf16[576,768]{1,0:T(8,128)(2,1)}, u32[]{:S(2)}, u32[]{:S(2)}) collective-permute-start(bf16[576,768]{1,0:T(8,128)(2,1)} %bitcast.54), channel_id=1, source_target_pairs={{0,8},{1,17},{2,10},{3,19},{4,12},{5,21},{6,14},{7,23},{8,0},{9,25... | collective-permute-start | bytes 2654216 | tf_op jit(solution)/shard_map/ppermute | solution.py:40
  13.1 1.7 %collective-permute-start.1 = (bf16[32,896]{1,0:T(8,128)(2,1)S(1)}, bf16[32,896]{1,0:T(8,128)(2,1)S(1)}, u32[]{:S(2)}, u32[]{:S(2)}) collective-permute-start(bf16[32,896]{1,0:T(8,128)(2,1)S(1)} %pad_maximum_fusion.7), channel_id=1, source_target_pairs={{0,16},{8,24},{16,0},{24,8},{1,17},{9,25},{17,1},{25,9},{2,18},{10... | collective-permute-start | bytes 172040 | tf_op jit(solution)/shard_map/ppermute | solution.py:26
  14.8 2.3 %collective-permute-done.7 = bf16[336,256]{1,0:T(8,128)(2,1)} collective-permute-done((bf16[336,256]{1,0:T(8,128)(2,1)S(1)}, bf16[336,256]{1,0:T(8,128)(2,1)}, u32[]{:S(2)}, u32[]{:S(2)}) %collective-permute-start.7) | collective-permute-done | bytes 172064 | tf_op jit(solution)/shard_map/ppermute | solution.py:31
  17.1 2.4 %collective-permute-start.5 = (bf16[576,384]{1,0:T(8,128)(2,1)S(1)}, bf16[576,384]{1,0:T(8,128)(2,1)}, u32[]{:S(2)}, u32[]{:S(2)}) collective-permute-start(bf16[576,384]{1,0:T(8,128)(2,1)S(1)} %dynamic-slice_bitcast_fusion), channel_id=1, source_target_pairs={{0,24},{8,16},{16,8},{24,0},{1,25},{9,17},{17,9},{25,1},{2,26},{10... | collective-permute-start | bytes 1327112 | tf_op jit(solution)/shard_map/ppermute | solution.py:26
  19.5 4.3 %collective-permute-done.3.refs_4_ = bf16[576,768]{1,0:T(8,128)(2,1)} collective-permute-done((bf16[576,768]{1,0:T(8,128)(2,1)}, bf16[576,768]{1,0:T(8,128)(2,1)}, u32[]{:S(2)}, u32[]{:S(2)}) %collective-permute-start.3) | collective-permute-done | bytes 884768 | tf_op jit(solution)/shard_map/ppermute | solution.py:40
  26.2 3.1 %collective-permute-start.2 = (bf16[32,896]{1,0:T(8,128)(2,1)S(1)}, bf16[32,896]{1,0:T(8,128)(2,1)S(1)}, u32[]{:S(2)}, u32[]{:S(2)}) collective-permute-start(bf16[32,896]{1,0:T(8,128)(2,1)S(1)} %pad_maximum_fusion.7), channel_id=1, source_target_pairs={{0,24},{8,16},{16,8},{24,0},{1,25},{9,17},{17,9},{25,1},{2,26},{10... | collective-permute-start | bytes 172040 | tf_op jit(solution)/shard_map/ppermute | solution.py:26
  29.4 6.5 %collective-permute-done.2 = bf16[32,896]{1,0:T(8,128)(2,1)S(1)} collective-permute-done((bf16[32,896]{1,0:T(8,128)(2,1)S(1)}, bf16[32,896]{1,0:T(8,128)(2,1)S(1)}, u32[]{:S(2)}, u32[]{:S(2)}) %collective-permute-start.2) | collective-permute-done | bytes 57376 | tf_op jit(solution)/shard_map/ppermute | solution.py:26
  35.9 1.5 %collective-permute-start.11 = (bf16[192,768]{1,0:T(8,128)(2,1)S(1)}, bf16[192,768]{1,0:T(8,128)(2,1)S(1)}, u32[]{:S(2)}, u32[]{:S(2)}) collective-permute-start(bf16[192,768]{1,0:T(8,128)(2,1)S(1)} %bitcast.52), channel_id=1, source_target_pairs={{0,8},{1,17},{2,10},{3,19},{4,12},{5,21},{6,14},{7,23},{8,0},{9,25... | collective-permute-start | bytes 884744 | tf_op jit(solution)/shard_map/ppermute | solution.py:40
  37.9 1.6 %collective-permute-done.6.refs_7_ = bf16[576,384]{1,0:T(8,128)(2,1)S(1)} collective-permute-done((bf16[576,384]{1,0:T(8,128)(2,1)}, bf16[576,384]{1,0:T(8,128)(2,1)S(1)}, u32[]{:S(2)}, u32[]{:S(2)}) %collective-permute-start.6) | collective-permute-done | bytes 442400 | tf_op jit(solution)/shard_map/ppermute | solution.py:31
  41.2 9.4 %attention.1 = (f32[16,768]{1,0:T(8,128)}, f32[16,768]{1,0:T(8,128)}, bf16[2,768,256]{2,1,0:T(8,128)(2,1)}, bf16[2,192,768]{2,1,0:T(8,128)(2,1)}) custom-call(bf16[512,768]{1,0:T(8,128)(2,1)} %fusion.5.refs_0_, s32[4,128]{1,0:T(4,128)} %refs_1_.1, s32[128,4]{1,0:T(8,128)} %bitcast.57, bf16[576,768]{1,0:T(8,128)(2,1)} %bitcast.55, ...), custom_call_target="tpu_custom_call" | custom-call | flops 2113929216 | bytes 4718592 | tf_op jit(solution)/shard_map/attention/pallas_call | solution.py:227
  56.2 2.3 %collective-permute-start.17 = (bf16[16,768]{1,0:T(8,128)(2,1)S(1)}, bf16[16,768]{1,0:T(8,128)(2,1)S(1)}, u32[]{:S(2)}, u32[]{:S(2)}) collective-permute-start(bf16[16,768]{1,0:T(8,128)(2,1)S(1)} %add_convert_fusion), channel_id=1, source_target_pairs={{0,24},{8,16},{16,8},{24,0},{1,25},{9,17},{17,9},{25,1},{2,26},{10... | collective-permute-start | bytes 73736 | tf_op jit(solution)/shard_map/ppermute | solution.py:26
  59.4 2.2 %collective-permute-start.23 = (bf16[80,384]{1,0:T(8,128)(2,1)S(1)}, bf16[80,384]{1,0:T(8,128)(2,1)S(1)}, u32[]{:S(2)}, u32[]{:S(2)}) collective-permute-start(bf16[80,384]{1,0:T(8,128)(2,1)S(1)} %fusion.20), channel_id=1, source_target_pairs={{0,4},{1,5},{2,6},{3,7},{4,0},{5,1},{6,2},{7,3},{8,12},{9,13},{10,... | collective-permute-start | bytes 184328 | tf_op jit(solution)/shard_map/ppermute | solution.py:31
  61.7 1.5 %collective-permute-start.24 = (bf16[80,384]{1,0:T(8,128)(2,1)S(1)}, bf16[80,384]{1,0:T(8,128)(2,1)S(1)}, u32[]{:S(2)}, u32[]{:S(2)}) collective-permute-start(bf16[80,384]{1,0:T(8,128)(2,1)S(1)} %fusion.20), channel_id=1, source_target_pairs={{0,6},{1,7},{2,4},{3,5},{4,2},{5,3},{6,0},{7,1},{8,14},{9,15},{10,... | collective-permute-start | bytes 184328 | tf_op jit(solution)/shard_map/ppermute | solution.py:31
  63.7 2.9 %collective-permute-start.19 = (bf16[64,384]{1,0:T(8,128)(2,1)S(1)}, bf16[64,384]{1,0:T(8,128)(2,1)S(1)}, u32[]{:S(2)}, u32[]{:S(2)}) collective-permute-start(bf16[64,384]{1,0:T(8,128)(2,1)S(1)} %convert_element_type.60), channel_id=1, source_target_pairs={{0,4},{1,5},{2,6},{3,7},{4,0},{5,1},{6,2},{7,3},{8,12},{9,13},{10,... | collective-permute-start | bytes 147464 | tf_op jit(solution)/shard_map/ppermute | solution.py:31
  66.6 1.5 %collective-permute-start.20 = (bf16[64,384]{1,0:T(8,128)(2,1)S(1)}, bf16[64,384]{1,0:T(8,128)(2,1)S(1)}, u32[]{:S(2)}, u32[]{:S(2)}) collective-permute-start(bf16[64,384]{1,0:T(8,128)(2,1)S(1)} %convert_element_type.60), channel_id=1, source_target_pairs={{0,6},{1,7},{2,4},{3,5},{4,2},{5,3},{6,0},{7,1},{8,14},{9,15},{10,... | collective-permute-start | bytes 147464 | tf_op jit(solution)/shard_map/ppermute | solution.py:31
  68.5 2.2 %collective-permute-done.19 = bf16[64,384]{1,0:T(8,128)(2,1)S(1)} collective-permute-done((bf16[64,384]{1,0:T(8,128)(2,1)S(1)}, bf16[64,384]{1,0:T(8,128)(2,1)S(1)}, u32[]{:S(2)}, u32[]{:S(2)}) %collective-permute-start.19) | collective-permute-done | bytes 49184 | tf_op jit(solution)/shard_map/ppermute | solution.py:31
  70.7 1.7 %collective-permute-done.20 = bf16[64,384]{1,0:T(8,128)(2,1)S(1)} collective-permute-done((bf16[64,384]{1,0:T(8,128)(2,1)S(1)}, bf16[64,384]{1,0:T(8,128)(2,1)S(1)}, u32[]{:S(2)}, u32[]{:S(2)}) %collective-permute-start.20) | collective-permute-done | bytes 49184 | tf_op jit(solution)/shard_map/ppermute | solution.py:31
  73.3 2.7 %structure.1 = (bf16[4,256,256]{2,1,0:T(8,128)(2,1)}, bf16[8,128,64]{2,1,0:T(8,128)(2,1)}) custom-call(bf16[4,80,384]{2,1,0:T(8,128)(2,1)} %copy-done.4, bf16[4,80,384]{2,1,0:T(8,128)(2,1)} %copy-done.21), custom_call_target="tpu_custom_call" | custom-call | flops 1000000000 | bytes 1000000 | tf_op jit(solution)/shard_map/structure/pallas_call | solution.py:391
  76.7 5.4 %nodes.1 = (bf16[48,768]{1,0:T(8,128)(2,1)}, bf16[48,768]{1,0:T(8,128)(2,1)}, bf16[48,768]{1,0:T(8,128)(2,1)}, f32[48,768]{1,0:T(8,128)}, f32[32,128]{1,0:T(8,128)}) custom-call(bf16[4,64,384]{2,1,0:T(8,128)(2,1)} %copy-done.7, bf16[4,64,384]{2,1,0:T(8,128)(2,1)} %copy-done.22, bf16[4,80,384]{2,1,0:T(8,128)(2,1)} %copy-done.4, ...), custom_call_target="tpu_custom_call" | custom-call | flops 1000000000 | bytes 1000000 | tf_op jit(solution)/shard_map/nodes/pallas_call | solution.py:411
  82.5 1.5 %collective-permute-start.27 = (bf16[48,768]{1,0:T(8,128)(2,1)}, bf16[48,768]{1,0:T(8,128)(2,1)S(1)}, u32[]{:S(2)}, u32[]{:S(2)}) collective-permute-start(bf16[48,768]{1,0:T(8,128)(2,1)} %get-tuple-element.32), channel_id=1, source_target_pairs={{0,16},{8,24},{16,0},{24,8},{1,17},{9,25},{17,1},{25,9},{2,18},{10... | collective-permute-start | bytes 221192 | tf_op jit(solution)/shard_map/ppermute | solution.py:26
  83.9 1.6 %collective-permute-start.28 = (bf16[48,768]{1,0:T(8,128)(2,1)}, bf16[48,768]{1,0:T(8,128)(2,1)S(1)}, u32[]{:S(2)}, u32[]{:S(2)}) collective-permute-start(bf16[48,768]{1,0:T(8,128)(2,1)} %get-tuple-element.33), channel_id=1, source_target_pairs={{0,24},{8,16},{16,8},{24,0},{1,25},{9,17},{17,9},{25,1},{2,26},{10... | collective-permute-start | bytes 221192 | tf_op jit(solution)/shard_map/ppermute | solution.py:26
  88.0 1.7 %collective-permute-done.28.refs_2_ = bf16[48,768]{1,0:T(8,128)(2,1)S(1)} collective-permute-done((bf16[48,768]{1,0:T(8,128)(2,1)}, bf16[48,768]{1,0:T(8,128)(2,1)S(1)}, u32[]{:S(2)}, u32[]{:S(2)}) %collective-permute-start.28) | collective-permute-done | bytes 73760 | tf_op jit(solution)/shard_map/ppermute | solution.py:26
  90.3 1.7 %combine.1 = (bf16[32,768]{1,0:T(8,128)(2,1)}, bf16[16,768]{1,0:T(8,128)(2,1)}) custom-call(f32[48,768]{1,0:T(8,128)} %get-tuple-element.29.own, f32[32,128]{1,0:T(8,128)} %get-tuple-element.30.live, bf16[48,768]{1,0:T(8,128)(2,1)} %copy-done.8, bf16[48,768]{1,0:T(8,128)(2,1)} %copy-done.9, bf16[48,768]{1,0:T(8,128)(2,1)} %copy-done.10), custom_call_target="tpu_custom_call" | custom-call | tf_op jit(solution)/shard_map/combine/pallas_call | solution.py:440
  (148 shorter events, 22.6 us)
Async XLA Ops:
  2.7 10.4 %collective-permute-start.9 = (bf16[336,256]{1,0:T(8,128)(2,1)S(1)}, bf16[336,256]{1,0:T(8,128)(2,1)S(1)}, u32[]{:S(2)}, u32[]{:S(2)}) collective-permute-start(bf16[336,256]{1,0:T(8,128)(2,1)S(1)} %get-tuple-element.46), channel_id=1, source_target_pairs={{0,6},{1,7},{2,4},{3,5},{4,2},{5,3},{6,0},{7,1},{8,14},{9,15},{10,... | collective-permute-start | bytes 516104 | tf_op jit(solution)/shard_map/ppermute | solution.py:31
  7.9 9.2 %collective-permute-start.7 = (bf16[336,256]{1,0:T(8,128)(2,1)S(1)}, bf16[336,256]{1,0:T(8,128)(2,1)}, u32[]{:S(2)}, u32[]{:S(2)}) collective-permute-start(bf16[336,256]{1,0:T(8,128)(2,1)S(1)} %get-tuple-element.46), channel_id=1, source_target_pairs={{0,2},{1,3},{2,0},{3,1},{4,6},{5,7},{6,4},{7,5},{8,10},{9,11},{10,... | collective-permute-start | bytes 516104 | tf_op jit(solution)/shard_map/ppermute | solution.py:31
  7.9 15.9 %collective-permute-start.8 = (bf16[336,256]{1,0:T(8,128)(2,1)S(1)}, bf16[336,256]{1,0:T(8,128)(2,1)}, u32[]{:S(2)}, u32[]{:S(2)}) collective-permute-start(bf16[336,256]{1,0:T(8,128)(2,1)S(1)} %get-tuple-element.46), channel_id=1, source_target_pairs={{0,4},{1,5},{2,6},{3,7},{4,0},{5,1},{6,2},{7,3},{8,12},{9,13},{10,... | collective-permute-start | bytes 516104 | tf_op jit(solution)/shard_map/ppermute | solution.py:31
  8.5 15.3 %collective-permute-start.3 = (bf16[576,768]{1,0:T(8,128)(2,1)}, bf16[576,768]{1,0:T(8,128)(2,1)}, u32[]{:S(2)}, u32[]{:S(2)}) collective-permute-start(bf16[576,768]{1,0:T(8,128)(2,1)} %bitcast.54), channel_id=1, source_target_pairs={{0,8},{1,17},{2,10},{3,19},{4,12},{5,21},{6,14},{7,23},{8,0},{9,25... | collective-permute-start | bytes 2654216 | tf_op jit(solution)/shard_map/ppermute | solution.py:40
  10.5 15.7 %collective-permute-start = (bf16[32,896]{1,0:T(8,128)(2,1)S(1)}, bf16[32,896]{1,0:T(8,128)(2,1)S(1)}, u32[]{:S(2)}, u32[]{:S(2)}) collective-permute-start(bf16[32,896]{1,0:T(8,128)(2,1)S(1)} %pad_maximum_fusion.7), channel_id=1, source_target_pairs={{0,8},{8,0},{16,24},{24,16},{1,9},{9,1},{17,25},{25,17},{2,10},{10... | collective-permute-start | bytes 172040 | tf_op jit(solution)/shard_map/ppermute | solution.py:26
  13.1 16.1 %collective-permute-start.1 = (bf16[32,896]{1,0:T(8,128)(2,1)S(1)}, bf16[32,896]{1,0:T(8,128)(2,1)S(1)}, u32[]{:S(2)}, u32[]{:S(2)}) collective-permute-start(bf16[32,896]{1,0:T(8,128)(2,1)S(1)} %pad_maximum_fusion.7), channel_id=1, source_target_pairs={{0,16},{8,24},{16,0},{24,8},{1,17},{9,25},{17,1},{25,9},{2,18},{10... | collective-permute-start | bytes 172040 | tf_op jit(solution)/shard_map/ppermute | solution.py:26
  17.1 20.4 %collective-permute-start.5 = (bf16[576,384]{1,0:T(8,128)(2,1)S(1)}, bf16[576,384]{1,0:T(8,128)(2,1)}, u32[]{:S(2)}, u32[]{:S(2)}) collective-permute-start(bf16[576,384]{1,0:T(8,128)(2,1)S(1)} %dynamic-slice_bitcast_fusion), channel_id=1, source_target_pairs={{0,24},{8,16},{16,8},{24,0},{1,25},{9,17},{17,9},{25,1},{2,26},{10... | collective-permute-start | bytes 1327112 | tf_op jit(solution)/shard_map/ppermute | solution.py:26
  23.8 15.7 %collective-permute-start.4 = (bf16[576,768]{1,0:T(8,128)(2,1)}, bf16[576,768]{1,0:T(8,128)(2,1)S(1)}, u32[]{:S(2)}, u32[]{:S(2)}) collective-permute-start(bf16[576,768]{1,0:T(8,128)(2,1)} %collective-permute-done.3.refs_4_), channel_id=1, source_target_pairs={{0,1},{1,0},{2,3},{3,2},{4,5},{5,4},{6,7},{7,6},{8,9},{9,8},{10,11... | collective-permute-start | bytes 2654216 | tf_op jit(solution)/shard_map/ppermute | solution.py:31
  24.9 13.0 %collective-permute-start.10 = (bf16[4,336,256]{2,1,0:T(8,128)(2,1)S(1)}, bf16[4,336,256]{2,1,0:T(8,128)(2,1)}, u32[]{:S(2)}, u32[]{:S(2)}) collective-permute-start(bf16[4,336,256]{2,1,0:T(8,128)(2,1)S(1)} %pad_maximum_fusion.2.refs_8_), channel_id=1, source_target_pairs={{0,1},{1,0},{2,3},{3,2},{4,5},{5,4},{6,7},{7,6},{8,9},{9,8},{10,11... | collective-permute-start | bytes 2064392 | tf_op jit(solution)/shard_map/ppermute | solution.py:31
  26.2 9.7 %collective-permute-start.2 = (bf16[32,896]{1,0:T(8,128)(2,1)S(1)}, bf16[32,896]{1,0:T(8,128)(2,1)S(1)}, u32[]{:S(2)}, u32[]{:S(2)}) collective-permute-start(bf16[32,896]{1,0:T(8,128)(2,1)S(1)} %pad_maximum_fusion.7), channel_id=1, source_target_pairs={{0,24},{8,16},{16,8},{24,0},{1,25},{9,17},{17,9},{25,1},{2,26},{10... | collective-permute-start | bytes 172040 | tf_op jit(solution)/shard_map/ppermute | solution.py:26
  29.3 21.3 %collective-permute-start.12 = (bf16[192,384]{1,0:T(8,128)(2,1)S(1)}, bf16[192,384]{1,0:T(8,128)(2,1)S(1)}, u32[]{:S(2)}, u32[]{:S(2)}) collective-permute-start(bf16[192,384]{1,0:T(8,128)(2,1)S(1)} %dynamic-slice_bitcast_fusion.1), channel_id=1, source_target_pairs={{0,24},{8,16},{16,8},{24,0},{1,25},{9,17},{17,9},{25,1},{2,26},{10... | collective-permute-start | bytes 442376 | tf_op jit(solution)/shard_map/ppermute | solution.py:26
  35.9 14.7 %collective-permute-start.11 = (bf16[192,768]{1,0:T(8,128)(2,1)S(1)}, bf16[192,768]{1,0:T(8,128)(2,1)S(1)}, u32[]{:S(2)}, u32[]{:S(2)}) collective-permute-start(bf16[192,768]{1,0:T(8,128)(2,1)S(1)} %bitcast.52), channel_id=1, source_target_pairs={{0,8},{1,17},{2,10},{3,19},{4,12},{5,21},{6,14},{7,23},{8,0},{9,25... | collective-permute-start | bytes 884744 | tf_op jit(solution)/shard_map/ppermute | solution.py:40
  55.0 6.7 %collective-permute-start.15 = (bf16[16,768]{1,0:T(8,128)(2,1)S(1)}, bf16[16,768]{1,0:T(8,128)(2,1)S(1)}, u32[]{:S(2)}, u32[]{:S(2)}) collective-permute-start(bf16[16,768]{1,0:T(8,128)(2,1)S(1)} %add_convert_fusion), channel_id=1, source_target_pairs={{0,8},{8,0},{16,24},{24,16},{1,9},{9,1},{17,25},{25,17},{2,10},{10... | collective-permute-start | bytes 73736 | tf_op jit(solution)/shard_map/ppermute | solution.py:26
  55.6 7.6 %collective-permute-start.16 = (bf16[16,768]{1,0:T(8,128)(2,1)S(1)}, bf16[16,768]{1,0:T(8,128)(2,1)S(1)}, u32[]{:S(2)}, u32[]{:S(2)}) collective-permute-start(bf16[16,768]{1,0:T(8,128)(2,1)S(1)} %add_convert_fusion), channel_id=1, source_target_pairs={{0,16},{8,24},{16,0},{24,8},{1,17},{9,25},{17,1},{25,9},{2,18},{10... | collective-permute-start | bytes 73736 | tf_op jit(solution)/shard_map/ppermute | solution.py:26
  56.2 6.9 %collective-permute-start.17 = (bf16[16,768]{1,0:T(8,128)(2,1)S(1)}, bf16[16,768]{1,0:T(8,128)(2,1)S(1)}, u32[]{:S(2)}, u32[]{:S(2)}) collective-permute-start(bf16[16,768]{1,0:T(8,128)(2,1)S(1)} %add_convert_fusion), channel_id=1, source_target_pairs={{0,24},{8,16},{16,8},{24,0},{1,25},{9,17},{17,9},{25,1},{2,26},{10... | collective-permute-start | bytes 73736 | tf_op jit(solution)/shard_map/ppermute | solution.py:26
  58.7 7.9 %collective-permute-start.22 = (bf16[80,384]{1,0:T(8,128)(2,1)S(1)}, bf16[80,384]{1,0:T(8,128)(2,1)S(1)}, u32[]{:S(2)}, u32[]{:S(2)}) collective-permute-start(bf16[80,384]{1,0:T(8,128)(2,1)S(1)} %fusion.20), channel_id=1, source_target_pairs={{0,2},{1,3},{2,0},{3,1},{4,6},{5,7},{6,4},{7,5},{8,10},{9,11},{10,... | collective-permute-start | bytes 184328 | tf_op jit(solution)/shard_map/ppermute | solution.py:31
  59.4 8.6 %collective-permute-start.23 = (bf16[80,384]{1,0:T(8,128)(2,1)S(1)}, bf16[80,384]{1,0:T(8,128)(2,1)S(1)}, u32[]{:S(2)}, u32[]{:S(2)}) collective-permute-start(bf16[80,384]{1,0:T(8,128)(2,1)S(1)} %fusion.20), channel_id=1, source_target_pairs={{0,4},{1,5},{2,6},{3,7},{4,0},{5,1},{6,2},{7,3},{8,12},{9,13},{10,... | collective-permute-start | bytes 184328 | tf_op jit(solution)/shard_map/ppermute | solution.py:31
  61.7 6.6 %collective-permute-start.24 = (bf16[80,384]{1,0:T(8,128)(2,1)S(1)}, bf16[80,384]{1,0:T(8,128)(2,1)S(1)}, u32[]{:S(2)}, u32[]{:S(2)}) collective-permute-start(bf16[80,384]{1,0:T(8,128)(2,1)S(1)} %fusion.20), channel_id=1, source_target_pairs={{0,6},{1,7},{2,4},{3,5},{4,2},{5,3},{6,0},{7,1},{8,14},{9,15},{10,... | collective-permute-start | bytes 184328 | tf_op jit(solution)/shard_map/ppermute | solution.py:31
  63.6 5.0 %collective-permute-start.18 = (bf16[64,384]{1,0:T(8,128)(2,1)S(1)}, bf16[64,384]{1,0:T(8,128)(2,1)S(1)}, u32[]{:S(2)}, u32[]{:S(2)}) collective-permute-start(bf16[64,384]{1,0:T(8,128)(2,1)S(1)} %convert_element_type.60), channel_id=1, source_target_pairs={{0,2},{1,3},{2,0},{3,1},{4,6},{5,7},{6,4},{7,5},{8,10},{9,11},{10,... | collective-permute-start | bytes 147464 | tf_op jit(solution)/shard_map/ppermute | solution.py:31
  63.7 7.1 %collective-permute-start.19 = (bf16[64,384]{1,0:T(8,128)(2,1)S(1)}, bf16[64,384]{1,0:T(8,128)(2,1)S(1)}, u32[]{:S(2)}, u32[]{:S(2)}) collective-permute-start(bf16[64,384]{1,0:T(8,128)(2,1)S(1)} %convert_element_type.60), channel_id=1, source_target_pairs={{0,4},{1,5},{2,6},{3,7},{4,0},{5,1},{6,2},{7,3},{8,12},{9,13},{10,... | collective-permute-start | bytes 147464 | tf_op jit(solution)/shard_map/ppermute | solution.py:31
  66.6 5.9 %collective-permute-start.20 = (bf16[64,384]{1,0:T(8,128)(2,1)S(1)}, bf16[64,384]{1,0:T(8,128)(2,1)S(1)}, u32[]{:S(2)}, u32[]{:S(2)}) collective-permute-start(bf16[64,384]{1,0:T(8,128)(2,1)S(1)} %convert_element_type.60), channel_id=1, source_target_pairs={{0,6},{1,7},{2,4},{3,5},{4,2},{5,3},{6,0},{7,1},{8,14},{9,15},{10,... | collective-permute-start | bytes 147464 | tf_op jit(solution)/shard_map/ppermute | solution.py:31
  82.0 4.9 %collective-permute-start.26 = (bf16[48,768]{1,0:T(8,128)(2,1)}, bf16[48,768]{1,0:T(8,128)(2,1)S(1)}, u32[]{:S(2)}, u32[]{:S(2)}) collective-permute-start(bf16[48,768]{1,0:T(8,128)(2,1)} %get-tuple-element.31), channel_id=1, source_target_pairs={{0,8},{8,0},{16,24},{24,16},{1,9},{9,1},{17,25},{25,17},{2,10},{10... | collective-permute-start | bytes 221192 | tf_op jit(solution)/shard_map/ppermute | solution.py:26
  82.5 5.5 %collective-permute-start.27 = (bf16[48,768]{1,0:T(8,128)(2,1)}, bf16[48,768]{1,0:T(8,128)(2,1)S(1)}, u32[]{:S(2)}, u32[]{:S(2)}) collective-permute-start(bf16[48,768]{1,0:T(8,128)(2,1)} %get-tuple-element.32), channel_id=1, source_target_pairs={{0,16},{8,24},{16,0},{24,8},{1,17},{9,25},{17,1},{25,9},{2,18},{10... | collective-permute-start | bytes 221192 | tf_op jit(solution)/shard_map/ppermute | solution.py:26
  83.9 5.8 %collective-permute-start.28 = (bf16[48,768]{1,0:T(8,128)(2,1)}, bf16[48,768]{1,0:T(8,128)(2,1)S(1)}, u32[]{:S(2)}, u32[]{:S(2)}) collective-permute-start(bf16[48,768]{1,0:T(8,128)(2,1)} %get-tuple-element.33), channel_id=1, source_target_pairs={{0,24},{8,16},{16,8},{24,0},{1,25},{9,17},{17,9},{25,1},{2,26},{10... | collective-permute-start | bytes 221192 | tf_op jit(solution)/shard_map/ppermute | solution.py:26
  (32 other events, 159.5 us)
